TPU v7x, 32 devices: a whole 2x2x4 slice. The times are simulated.
32 devices in a mesh: dom: 16 (over z, y, core), sub: 2 (over x).
Axes of the slice: x: 2, y: 2, z: 4, core: 2. Of those that a mesh axis runs over, the one named last changes fastest.
Arguments:
- fine_partial: float32 [2, 165, 2048], P('sub', None, 'dom'), may hold values from -6 to 6
- upward_ops: float32 [8, 165, 165], replicated, may hold values from -0.15625 to 0.15625
- interaction_ops: float32 [188, 165, 165], P('sub'), may hold values from -0.03125 to 0.03125
- downward_ops: float32 [8, 165, 165], replicated, may hold values from -0.5 to 0.5
- fine_list: int32 [188, 2048], P('sub', 'dom'), may hold values from -1 to 2047, as said below
- mid_list: int32 [188, 256], P('sub', 'dom'), may hold values from -1 to 255, as said below
- top_list: int32 [188, 32], P('sub', 'dom'), may hold values from -1 to 31, as said below
- upper_list: int32 [188, 4], P('sub'), may hold values from -1 to 3, as said below
- positions: float32 [3, 65536], P(None, ('dom', 'sub')), may hold values from -0.5 to 0.5
- leaf_cell: int32 [65536], P(('dom', 'sub')), may hold values from 0 to 2047, as said below
Outputs:
- local_fine: float32 [165, 2048], P(None, 'dom')
- potential: float32 [65536], P(('dom', 'sub'))
Inputs may be any that keep to these rules, and one draw needn't show every extreme that they name: `fine_list`: column t lists for each offset slot a cell of the finest level within 128 cells of t in Peano order, or -1 for an empty slot. `mid_list`: column t lists for each offset slot a cell of the middle level within 16 cells of t, or -1 for an empty slot. `top_list`: each entry is a cell of the top level, or -1 for an empty slot. `upper_list`: each entry is a cell of the upper level, or -1 for an empty slot. `leaf_cell`: A particle's leaf is one of the 128 finest cells owned by its own slab.
All inputs are finite; a program needn't handle non-finite values.
Results may differ from a plain program's by a relative error of at most 0.0003.
Values sent between devices are 32-bit elements; how exact they have to be, the bound alone decides.
A program may use at most 128 MiB of HBM per device.

v0:
```python
import functools

import jax
import jax.numpy as jnp
from jax import lax
from jax.experimental import pallas as pl
from jax.experimental.pallas import tpu as pltpu
from jax.sharding import PartitionSpec as P

ORDER = 8
LANES = 128


precise = lax.Precision.HIGHEST


def round_up(count, unit):
    return -(-count // unit) * unit


def exponents():
    entries = []
    for degree in range(ORDER + 1):
        for along_x in range(degree, -1, -1):
            for along_y in range(degree - along_x, -1, -1):
                entries.append((along_x, along_y, degree - along_x - along_y))
    return entries


def halves(value):
    high = value.astype(jnp.bfloat16)
    low = (value - high.astype(jnp.float32)).astype(jnp.bfloat16)
    return high, low


def one_hot(row, count):
    places = lax.broadcasted_iota(jnp.int32, (count, row.shape[1]), 0)
    return jnp.where(places == row, 1.0, 0.0).astype(jnp.bfloat16)


def interact_kernel(
    coeffs, slots, group, fine_ref, coarse_ref, fine_list, coarse_list, ops_ref, out_ref,
    fine_table, coarse_table, fine_picked, coarse_picked,
):
    rows = fine_ref.shape[0]
    depth = fine_list.shape[0]
    step = pl.program_id(0)

    @pl.when(step == 0)
    def _():
        for source, table in ((fine_ref, fine_table), (coarse_ref, coarse_table)):
            high, low = halves(source[...])
            table[...] = jnp.concatenate([high, low], axis=0)

        def pick(pair, carry):
            for table, entries, picked in (
                (fine_table, fine_list, fine_picked),
                (coarse_table, coarse_list, coarse_picked),
            ):
                chosen = jnp.concatenate(
                    [
                        one_hot(entries[pl.ds(2 * pair + k, 1), :], table.shape[1])
                        for k in range(2)
                    ],
                    axis=1,
                )
                both = jnp.dot(table[...], chosen, preferred_element_type=jnp.float32)
                value = both[:rows] + both[rows:]
                for k in range(2):
                    picked[pl.ds(2 * pair + k, rows, stride=depth), :] = value[
                        :, k * LANES : (k + 1) * LANES
                    ]
            return carry

        lax.fori_loop(0, depth // 2, pick, 0)
        out_ref[...] = jnp.zeros_like(out_ref)

    lane = lax.broadcasted_iota(jnp.int32, (rows, LANES), 1)
    filler = jnp.zeros((LANES - depth, 2 * LANES), jnp.bfloat16)
    for part in range(group // 8):
        block = jnp.swapaxes(ops_ref[:, 8 * part : 8 * part + 8, :], 0, 1)
        left = []
        right = []
        for k in range(8):
            term = step * group + 8 * part + k
            op = jnp.where((lane < slots) & (term < coeffs), block[k], 0.0)
            op_high, op_low = halves(op)
            start = pl.multiple_of(term * depth, 8)
            data = jnp.concatenate(
                [
                    fine_picked[pl.ds(start, depth), :],
                    coarse_picked[pl.ds(start, depth), :],
                ],
                axis=1,
            )
            high, low = halves(data)
            high = jnp.concatenate([high, filler], axis=0)
            low = jnp.concatenate([low, filler], axis=0)
            left += [op_high, op_high, op_low]
            right += [high, low, high]
        out_ref[...] += jnp.dot(
            jnp.concatenate(left, axis=1),
            jnp.concatenate(right, axis=0),
            preferred_element_type=jnp.float32,
        )


def interact(fine, coarse, fine_list, coarse_list, ops):
    coeffs, _, slots = ops.shape
    rows, width = fine.shape
    coarse_width = coarse.shape[1]
    depth = fine_list.shape[0]
    group = 24
    whole = lambda array: pl.BlockSpec(array.shape, lambda i: (0, 0))
    return pl.pallas_call(
        functools.partial(interact_kernel, coeffs, slots, group),
        grid=(rows // group,),
        in_specs=[
            whole(fine),
            whole(coarse),
            whole(fine_list),
            whole(coarse_list),
            pl.BlockSpec((rows, group, LANES), lambda i: (0, i, 0)),
        ],
        out_specs=pl.BlockSpec((rows, 2 * LANES), lambda i: (0, 0)),
        out_shape=jax.ShapeDtypeStruct((rows, 2 * LANES), jnp.float32),
        scratch_shapes=[
            pltpu.VMEM((2 * rows, width), jnp.bfloat16),
            pltpu.VMEM((2 * rows, coarse_width), jnp.bfloat16),
            pltpu.VMEM((rows * depth, LANES), jnp.float32),
            pltpu.VMEM((rows * depth, LANES), jnp.float32),
        ],
        compiler_params=pltpu.CompilerParams(vmem_limit_bytes=48 * 1024 * 1024),
        cost_estimate=pl.CostEstimate(
            flops=6 * rows * rows * LANES * 2 * LANES,
            bytes_accessed=4 * rows * rows * LANES,
            transcendentals=0,
        ),
    )(fine, coarse, fine_list, coarse_list, ops)


def potential_kernel(local_ref, leaf_ref, position_ref, exponent_ref, out_ref):
    rows, cells = local_ref.shape
    particles = leaf_ref.shape[1]
    high, low = halves(local_ref[...])
    table = jnp.concatenate([high, low], axis=0)
    masks = [
        [(exponent_ref[:, axis : axis + 1] // bit) % 2 == 1 for bit in (1, 2, 4, 8)]
        for axis in range(3)
    ]
    for start in range(0, particles, 2 * LANES):
        span = slice(start, start + 2 * LANES)
        chosen = one_hot(leaf_ref[:, span], cells)
        both = jnp.dot(table, chosen, preferred_element_type=jnp.float32)
        value = both[:rows] + both[rows:]
        for axis in range(3):
            power = position_ref[axis : axis + 1, span]
            for bit in range(4):
                value = value * jnp.where(masks[axis][bit], power, 1.0)
                power = power * power
        out_ref[:, span] = jnp.sum(value, axis=0, keepdims=True)


def evaluate(local, leaves, positions):
    rows = local.shape[0]
    table = jnp.asarray(exponents(), jnp.int32)
    table = jnp.pad(table, ((0, rows - table.shape[0]), (0, LANES - 3)))
    return pl.pallas_call(
        potential_kernel,
        out_shape=jax.ShapeDtypeStruct((1, leaves.shape[0]), jnp.float32),
        compiler_params=pltpu.CompilerParams(vmem_limit_bytes=32 * 1024 * 1024),
    )(local, leaves[None], positions, table)[0]


def upward(moments, upward_ops):
    parents = moments.shape[1] // 8
    grouped = moments.reshape(moments.shape[0], parents, 8)
    return jnp.einsum("oab,bpo->ap", upward_ops, grouped, precision=precise)


def downward(expansions, downward_ops):
    spread = jnp.einsum("oab,bp->apo", downward_ops, expansions, precision=precise)
    return spread.reshape(spread.shape[0], -1)


def settle(portion):
    count = lax.axis_size("sub")
    ring = [(i, (i + 1) % count) for i in range(count)]
    total = moving = portion
    for _ in range(count - 1):
        moving = lax.ppermute(moving, "sub", ring)
        total = total + moving
    return total


def extended(block):
    count = lax.axis_size("dom")
    forward = [(i, i + 1) for i in range(count - 1)]
    backward = [(target, source) for source, target in forward]
    low = lax.ppermute(block, "dom", forward)
    high = lax.ppermute(block, "dom", backward)
    return jnp.concatenate([low, block, high], axis=1)


def shards(
    fine_partial,
    upward_ops,
    interaction_ops,
    downward_ops,
    fine_list,
    mid_list,
    top_list,
    upper_list,
    positions,
    leaf_cell,
):
    slab_cells = fine_partial.shape[2]
    mid_cells = slab_cells // 8
    top_cells = slab_cells // 64
    domain = lax.axis_index("dom")
    slots, coeffs = interaction_ops.shape[:2]
    rows = round_up(coeffs, 24)
    depth = round_up(slots, 16)
    upper_span = max(1, top_cells // 8)
    upper_first = domain * top_cells // 8
    upper_sources = lax.dynamic_slice_in_dim(upper_list, upper_first, upper_span, 1)

    wide_fine = extended(settle(fine_partial[0]))
    wide_mid = upward(wide_fine, upward_ops)
    own_top = upward(wide_mid[:, mid_cells : 2 * mid_cells], upward_ops)
    top_moments = lax.all_gather(own_top, "dom", axis=1, tiled=True)
    upper_moments = upward(top_moments, upward_ops)

    def place(sources, offset):
        return jnp.where(sources >= 0, sources + offset, -1)

    def padded(array, height, width, fill):
        return jnp.pad(
            array,
            ((0, height - array.shape[0]), (0, width - array.shape[1])),
            constant_values=fill,
        )

    spread = wide_mid.shape[1]
    coarse = jnp.concatenate([wide_mid, top_moments, upper_moments], axis=1)
    coarse_sources = jnp.concatenate(
        [
            place(mid_list, mid_cells - domain * mid_cells),
            place(top_list, spread),
            place(upper_sources, spread + top_moments.shape[1]),
        ],
        axis=1,
    )
    fine_sources = place(fine_list, slab_cells - domain * slab_cells)
    terms = interact(
        padded(wide_fine, rows, wide_fine.shape[1], 0),
        padded(coarse, rows, round_up(coarse.shape[1], LANES), 0),
        padded(fine_sources, depth, LANES, -1),
        padded(coarse_sources, depth, LANES, -1),
        jnp.transpose(interaction_ops, (1, 2, 0)),
    )
    terms = settle(terms)[:coeffs]
    at = LANES
    mid_term = terms[:, at : at + mid_cells]
    at += mid_cells
    top_term = terms[:, at : at + top_cells]
    at += top_cells
    local_upper = terms[:, at : at + upper_span]
    down_top = downward(local_upper, downward_ops)
    top_offset = domain * top_cells % 8
    local_top = top_term + lax.dynamic_slice_in_dim(down_top, top_offset, top_cells, 1)
    local_mid = mid_term + downward(local_top, downward_ops)
    local_fine = terms[:, :slab_cells] + downward(local_mid, downward_ops)
    potential = evaluate(
        padded(local_fine, rows, slab_cells, 0), leaf_cell - domain * slab_cells, positions
    )
    return (local_fine, potential)


def solution(mesh):
    placed = (
        P("sub", None, "dom"),
        P(),
        P("sub", None, None),
        P(),
        P("sub", "dom"),
        P("sub", "dom"),
        P("sub", "dom"),
        P("sub", None),
        P(None, ("dom", "sub")),
        P(("dom", "sub")),
    )
    return jax.shard_map(
        shards,
        mesh=mesh,
        in_specs=placed,
        out_specs=(P(None, "dom"), P(("dom", "sub"))),
        check_vma=False,
    )
```

profile of v0, /device:TPU:0, one launch (start us, length us, event | category | flops | bytes accessed | tf_op | source)
XLA Modules:
  0.0 93.3 jit_solution(3310828781035661210)
XLA Ops:
  0.6 0.0 copy-start
  0.6 1.0 %copy.154 = f32[1,165,128]{2,1,0:T(8,128)S(1)} copy(f32[1,165,128]{2,0,1:T(1,128)} %param.11) | data formatting | bytes 168960
  1.6 3.0 %collective-permute-start = (f32[165,128]{1,0:T(8,128)S(1)}, f32[165,128]{1,0:T(8,128)S(1)}, u32[]{:S(2)}, u32[]{:S(2)}) collective-permute-start(f32[165,128]{1,0:T(8,128)S(1)} %bitcast.57), channel_id=1, source_target_pairs={{0,1},{1,0},{2,3},{3,2},{4,5},{5,4},{6,7},{7,6},{8,9},{9,8},{10,11... | collective-permute-start | bytes 253448 | tf_op jit(solution)/shard_map/ppermute | solution.py:191
  4.6 0.7 compare_select_fusion.1
  5.3 0.7 add_select_fusion.1
  6.0 0.8 add_select_fusion
  6.8 0.7 compare_select_fusion
  7.5 0.9 fusion.35
  8.4 1.5 %collective-permute-start.1 = (f32[165,128]{1,0:T(8,128)S(1)}, f32[165,128]{1,0:T(8,128)S(1)}, u32[]{:S(2)}, u32[]{:S(2)}) collective-permute-start(f32[165,128]{1,0:T(8,128)S(1)} %fusion.35), channel_id=1, source_target_pairs={{0,2},{2,4},{4,6},{6,8},{8,10},{10,12},{12,14},{14,16},{16,18},{18... | collective-permute-start | bytes 253448 | tf_op jit(solution)/shard_map/ppermute | solution.py:200
  9.9 1.3 %collective-permute-start.2 = (f32[165,128]{1,0:T(8,128)S(1)}, f32[165,128]{1,0:T(8,128)S(1)}, u32[]{:S(2)}, u32[]{:S(2)}) collective-permute-start(f32[165,128]{1,0:T(8,128)S(1)} %fusion.35), channel_id=1, source_target_pairs={{2,0},{4,2},{6,4},{8,6},{10,8},{12,10},{14,12},{16,14},{18,16},{20... | collective-permute-start | bytes 253448 | tf_op jit(solution)/shard_map/ppermute | solution.py:201
  11.2 0.1 copy.99
  11.3 3.4 %collective-permute-done.2 = f32[165,128]{1,0:T(8,128)S(1)} collective-permute-done((f32[165,128]{1,0:T(8,128)S(1)}, f32[165,128]{1,0:T(8,128)S(1)}, u32[]{:S(2)}, u32[]{:S(2)}) %collective-permute-start.2) | collective-permute-done | bytes 84512 | tf_op jit(solution)/shard_map/ppermute | solution.py:201
  14.8 0.2 copy.87
  14.9 1.5 %fusion.16 = f32[165,48]{1,0:T(8,128)S(1)} fusion(f32[8,165,165]{2,0,1:T(8,128)S(1)} %copy-done, f32[165,48,8]{0,2,1:T(8,128)S(1)} %bitcast.53), kind=kOutput, calls=%fused_computation.13 | convolution fusion | flops 125452800 | bytes 1156320 | tf_op jit(solution)/shard_map/oab,bpo->ap/dot_general | solution.py:178
  16.5 0.1 slice.25
  16.6 0.1 copy.91
  16.6 1.4 %fusion.22 = f32[1,2,165]{2,1,0:T(2,128)S(1)} fusion(f32[8,165,165]{2,0,1:T(8,128)S(1)} %copy-done, f32[165,2,8]{0,2,1:T(8,128)S(1)} %bitcast.58), kind=kOutput, calls=%fused_computation.15 | convolution fusion | flops 5227200 | bytes 883080 | tf_op jit(solution)/shard_map/oab,bpo->ap/dot_general | solution.py:178
  18.0 23.3 %all-gather = f32[16,2,165]{2,1,0:T(2,128)S(1)} all-gather(f32[1,2,165]{2,1,0:T(2,128)S(1)} %fusion.22), channel_id=1, replica_groups=mesh['dom'=16,'sub'=2] {'dom'}, dimensions={0}, use_global_device_ids=true | all-gather | bytes 22440 | tf_op jit(solution)/shard_map/all_gather | solution.py:231
  41.4 0.1 copy.94
  41.5 1.4 %fusion.13 = f32[165,4]{1,0:T(8,128)S(1)} fusion(f32[8,165,165]{2,0,1:T(8,128)S(1)} %copy-done, f32[165,4,8]{0,2,1:T(8,128)S(1)} %bitcast.56), kind=kOutput, calls=%fused_computation.12 | convolution fusion | flops 10454400 | bytes 894960 | tf_op jit(solution)/shard_map/oab,bpo->ap/dot_general | solution.py:178
  42.9 0.1 select_maximum_fusion.coarse_ref
  43.0 36.9 %shard_map.122 = f32[168,256]{1,0:T(8,128)S(1)} custom-call(f32[168,384]{1,0:T(8,128)S(1)} %pad.24.fine_ref, f32[168,128]{1,0:T(8,128)S(1)} %select_maximum_fusion.coarse_ref, s32[96,128]{1,0:T(8,128)S(1)} %pad.26.fine_list, s32[96,128]{1,0:T(8,128)S(1)} %pad.27.coarse_list, f32[165,165,94]{2,1,0:T(8,128)} %bitcast.61), custom_call_target="tpu_custom_call" | custom-call | flops 5549064192 | bytes 14450688 | tf_op jit(solution)/shard_map/pallas_call | solution.py:115
  80.0 1.6 %collective-permute-start.3 = (f32[168,256]{1,0:T(8,128)S(1)}, f32[168,256]{1,0:T(8,128)S(1)}, u32[]{:S(2)}, u32[]{:S(2)}) collective-permute-start(f32[168,256]{1,0:T(8,128)S(1)} %shard_map.122), channel_id=1, source_target_pairs={{0,1},{1,0},{2,3},{3,2},{4,5},{5,4},{6,7},{7,6},{8,9},{9,8},{10,11... | collective-permute-start | bytes 516104 | tf_op jit(solution)/shard_map/ppermute | solution.py:191
  81.5 5.1 %collective-permute-done.3 = f32[168,256]{1,0:T(8,128)S(1)} collective-permute-done((f32[168,256]{1,0:T(8,128)S(1)}, f32[168,256]{1,0:T(8,128)S(1)}, u32[]{:S(2)}, u32[]{:S(2)}) %collective-permute-start.3) | collective-permute-done | bytes 172064 | tf_op jit(solution)/shard_map/ppermute | solution.py:191
  86.7 0.2 slice_reduce_fusion
  86.9 0.3 multiply_reduce_fusion
  87.1 1.7 %fusion.19 = f32[165,2,8]{0,1,2:T(2,128)S(1)} fusion(f32[8,165,165]{2,0,1:T(8,128)S(1)} %copy-done.3, f32[168,256]{1,0:T(8,128)S(1)} %add.72, f32[8,165]{0,1:T(8,128)S(1)} %multiply_reduce_fusion, s32[]{:T(128)S(6)} %select_n.40), kind=kOutput, calls=%fused_computation.14 | convolution fusion | flops 5227530 | bytes 1534276 | tf_op jit(solution)/shard_map/oab,bp->apo/dot_general | solution.py:182
  88.8 0.1 copy.103
  88.9 1.6 %fusion.10 = f32[165,16,8]{0,1,2:T(8,128)S(1)} fusion(f32[8,165,165]{2,0,1:T(8,128)S(1)} %copy-done.3, f32[165,16]{1,0:T(8,128)S(1)} %copy.103, f32[168,256]{1,0:T(8,128)S(1)} %add.72), kind=kOutput, calls=%fused_computation.11 | convolution fusion | flops 41820240 | bytes 1608192 | tf_op jit(solution)/shard_map/oab,bp->apo/dot_general | solution.py:182
  90.5 0.1 copy.153
  90.6 0.1 copy.107
  90.8 2.5 %shard_map.123 = f32[1,2048]{1,0:T(1,128)} custom-call(f32[168,128]{1,0:T(8,128)S(1)} %pad.28.local_ref, s32[1,2048]{1,0:T(1,128)S(1)} %bitcast.52, f32[3,2048]{1,0:T(4,128)S(1)} %copy-done.2, s32[168,128]{1,0:T(8,128)S(1)} %copy-done.1), custom_call_target="tpu_custom_call" | custom-call | tf_op jit(solution)/shard_map/pallas_call | solution.py:168
  (24 shorter events, 0.2 us)
Async XLA Ops:
  0.6 14.3 %copy-start = (f32[8,165,165]{2,0,1:T(8,128)S(1)}, f32[8,165,165]{2,0,1:T(8,128)}, u32[]{:S(2)}) copy-start(f32[8,165,165]{2,0,1:T(8,128)} %param.12) | copy-start | bytes 2613604
  1.6 5.8 %collective-permute-start = (f32[165,128]{1,0:T(8,128)S(1)}, f32[165,128]{1,0:T(8,128)S(1)}, u32[]{:S(2)}, u32[]{:S(2)}) collective-permute-start(f32[165,128]{1,0:T(8,128)S(1)} %bitcast.57), channel_id=1, source_target_pairs={{0,1},{1,0},{2,3},{3,2},{4,5},{5,4},{6,7},{7,6},{8,9},{9,8},{10,11... | collective-permute-start | bytes 253448 | tf_op jit(solution)/shard_map/ppermute | solution.py:191
  8.4 2.9 %collective-permute-start.1 = (f32[165,128]{1,0:T(8,128)S(1)}, f32[165,128]{1,0:T(8,128)S(1)}, u32[]{:S(2)}, u32[]{:S(2)}) collective-permute-start(f32[165,128]{1,0:T(8,128)S(1)} %fusion.35), channel_id=1, source_target_pairs={{0,2},{2,4},{4,6},{6,8},{8,10},{10,12},{12,14},{14,16},{16,18},{18... | collective-permute-start | bytes 253448 | tf_op jit(solution)/shard_map/ppermute | solution.py:200
  9.9 4.9 %collective-permute-start.2 = (f32[165,128]{1,0:T(8,128)S(1)}, f32[165,128]{1,0:T(8,128)S(1)}, u32[]{:S(2)}, u32[]{:S(2)}) collective-permute-start(f32[165,128]{1,0:T(8,128)S(1)} %fusion.35), channel_id=1, source_target_pairs={{2,0},{4,2},{6,4},{8,6},{10,8},{12,10},{14,12},{16,14},{18,16},{20... | collective-permute-start | bytes 253448 | tf_op jit(solution)/shard_map/ppermute | solution.py:201
  43.0 38.5 %copy-start.5 = (s32[2048]{0:T(1024)S(1)}, s32[2048]{0:T(1024)}, u32[]{:S(2)}) copy-start(s32[2048]{0:T(1024)} %param.20) | copy-start | bytes 24580
  43.0 43.9 %copy-start.3 = (f32[8,165,165]{2,0,1:T(8,128)S(1)}, f32[8,165,165]{2,0,1:T(8,128)}, u32[]{:S(2)}) copy-start(f32[8,165,165]{2,0,1:T(8,128)} %param.14) | copy-start | bytes 2613604
  80.0 6.7 %collective-permute-start.3 = (f32[168,256]{1,0:T(8,128)S(1)}, f32[168,256]{1,0:T(8,128)S(1)}, u32[]{:S(2)}, u32[]{:S(2)}) collective-permute-start(f32[168,256]{1,0:T(8,128)S(1)} %shard_map.122), channel_id=1, source_target_pairs={{0,1},{1,0},{2,3},{3,2},{4,5},{5,4},{6,7},{7,6},{8,9},{9,8},{10,11... | collective-permute-start | bytes 516104 | tf_op jit(solution)/shard_map/ppermute | solution.py:191
  88.8 2.0 %copy-start.1 = (s32[168,128]{1,0:T(8,128)S(1)}, s32[168,128]{1,0:T(8,128)}, u32[]{:S(2)}) copy-start(s32[168,128]{1,0:T(8,128)} %constant.70.exponent_ref) | copy-start | bytes 258052
  88.8 2.0 %copy-start.2 = (f32[3,2048]{1,0:T(4,128)S(1)}, f32[3,2048]{1,0:T(4,128)}, u32[]{:S(2)}) copy-start(f32[3,2048]{1,0:T(4,128)} %position_ref.1) | copy-start | bytes 73732
  90.7 2.6 %copy-start.4 = (f32[165,128]{1,0:T(8,128)}, f32[165,128]{1,0:T(8,128)S(1)}, u32[]{:S(2)}) copy-start(f32[165,128]{1,0:T(8,128)S(1)} %slice_add_fusion.2) | copy-start | bytes 253444
where the time goes:
time: 93.8 us; the launch traced here: 93.3 us
  Pallas kernels  39.5 us (42%)
  blocking collectives  23.3 us (25%)
  waiting for transfers between devices  8.54 us (9%)
  matrix products  7.56 us (8%)
  starting transfers between devices  7.28 us (8%)
  other arithmetic  4.21 us (4%)
  local copies, waits for them, and re-layouts  2.09 us (2%)
    pallas_call x1, Pallas kernels, interact(): pl.pallas_call(functools.partial(interact_kernel, coeffs, slots, group),...  36.9 us
    all_gather x1, blocking collectives, shards(): top_moments = lax.all_gather(own_top, 'dom', axis=1, tiled=True)  23.3 us
    ppermute x2, waiting for transfers between devices, settle(): moving = lax.ppermute(moving, 'sub', ring)  5.13 us
    ppermute x2, starting transfers between devices, settle(): moving = lax.ppermute(moving, 'sub', ring)  4.52 us
    dot_general x3, matrix products, upward(): return jnp.einsum('oab,bpo->ap', upward_ops, grouped, precision=precise)  4.3 us
    ppermute x1, waiting for transfers between devices, extended(): high = lax.ppermute(block, 'dom', backward)  3.41 us
    dot_general x2, matrix products, downward(): jnp.einsum('oab,bp->apo', downward_ops, expansions, precision=precise)  3.26 us
    select_n x4, other arithmetic, place(): return jnp.where(sources >= 0, sources + offset, -1)  2.87 us
  transfers between devices with their start and end apart: 4, of which 2 were waited for; matrix products, arithmetic and copies ran while one was open for 3% of the time, Pallas kernels for 0%

commit v1 on v0

--- a/solution.py
+++ b/solution.py
@@ -52,27 +52,28 @@
             high, low = halves(source[...])
             table[...] = jnp.concatenate([high, low], axis=0)
 
-        def pick(pair, carry):
+        def pick(batch, carry):
+            base = pl.multiple_of(8 * batch, 8)
             for table, entries, picked in (
                 (fine_table, fine_list, fine_picked),
                 (coarse_table, coarse_list, coarse_picked),
             ):
-                chosen = jnp.concatenate(
-                    [
-                        one_hot(entries[pl.ds(2 * pair + k, 1), :], table.shape[1])
-                        for k in range(2)
-                    ],
-                    axis=1,
-                )
-                both = jnp.dot(table[...], chosen, preferred_element_type=jnp.float32)
-                value = both[:rows] + both[rows:]
-                for k in range(2):
-                    picked[pl.ds(2 * pair + k, rows, stride=depth), :] = value[
-                        :, k * LANES : (k + 1) * LANES
-                    ]
+                columns = []
+                for k in range(0, 8, 2):
+                    chosen = jnp.concatenate(
+                        [
+                            one_hot(entries[pl.ds(base + k + m, 1), :], table.shape[1])
+                            for m in range(2)
+                        ],
+                        axis=1,
+                    )
+                    both = jnp.dot(table[...], chosen, preferred_element_type=jnp.float32)
+                    value = both[:rows] + both[rows:]
+                    columns += [value[:, :LANES], value[:, LANES:]]
+                picked[:, pl.ds(base, 8), :] = jnp.swapaxes(jnp.stack(columns), 0, 1)
             return carry
 
-        lax.fori_loop(0, depth // 2, pick, 0)
+        lax.fori_loop(0, depth // 8, pick, 0)
         out_ref[...] = jnp.zeros_like(out_ref)
 
     lane = lax.broadcasted_iota(jnp.int32, (rows, LANES), 1)
@@ -85,14 +86,7 @@
             term = step * group + 8 * part + k
             op = jnp.where((lane < slots) & (term < coeffs), block[k], 0.0)
             op_high, op_low = halves(op)
-            start = pl.multiple_of(term * depth, 8)
-            data = jnp.concatenate(
-                [
-                    fine_picked[pl.ds(start, depth), :],
-                    coarse_picked[pl.ds(start, depth), :],
-                ],
-                axis=1,
-            )
+            data = jnp.concatenate([fine_picked[term], coarse_picked[term]], axis=1)
             high, low = halves(data)
             high = jnp.concatenate([high, filler], axis=0)
             low = jnp.concatenate([low, filler], axis=0)
@@ -127,8 +121,8 @@
         scratch_shapes=[
             pltpu.VMEM((2 * rows, width), jnp.bfloat16),
             pltpu.VMEM((2 * rows, coarse_width), jnp.bfloat16),
-            pltpu.VMEM((rows * depth, LANES), jnp.float32),
-            pltpu.VMEM((rows * depth, LANES), jnp.float32),
+            pltpu.VMEM((rows, depth, LANES), jnp.float32),
+            pltpu.VMEM((rows, depth, LANES), jnp.float32),
         ],
         compiler_params=pltpu.CompilerParams(vmem_limit_bytes=48 * 1024 * 1024),
         cost_estimate=pl.CostEstimate(

time: 93.8 us -> 78.3 us (0.83)
  Pallas kernels: 39.5 us -> 23.9 us
    pallas_call x1, Pallas kernels: 36.9 us -> 21.4 us  [interact(): pl.pallas_call(functools.partial(interact_kernel, coeffs, slots, group),...]
  transfers between devices with their start and end apart: 4 -> 4, of which waited for: 2 -> 2; matrix products, arithmetic and copies ran while one was open for 3% -> 4% of each run, Pallas kernels for 0% -> 0%
where the time goes in v1:
time: 78.3 us; the launch traced here: 77.8 us
  Pallas kernels  23.9 us (31%)
  blocking collectives  23.3 us (30%)
  waiting for transfers between devices  8.54 us (11%)
  matrix products  7.56 us (10%)
  starting transfers between devices  7.28 us (9%)
  other arithmetic  4.21 us (5%)
  local copies, waits for them, and re-layouts  2.09 us (3%)
  between operations  0.86 us (1%)
    all_gather x1, blocking collectives, shards(): top_moments = lax.all_gather(own_top, 'dom', axis=1, tiled=True)  23.3 us
    pallas_call x1, Pallas kernels, interact(): pl.pallas_call(functools.partial(interact_kernel, coeffs, slots, group),...  21.4 us
    ppermute x2, waiting for transfers between devices, settle(): moving = lax.ppermute(moving, 'sub', ring)  5.13 us
    ppermute x2, starting transfers between devices, settle(): moving = lax.ppermute(moving, 'sub', ring)  4.53 us
    dot_general x3, matrix products, upward(): return jnp.einsum('oab,bpo->ap', upward_ops, grouped, precision=precise)  4.3 us
    ppermute x1, waiting for transfers between devices, extended(): high = lax.ppermute(block, 'dom', backward)  3.41 us
    dot_general x2, matrix products, downward(): jnp.einsum('oab,bp->apo', downward_ops, expansions, precision=precise)  3.26 us
    select_n x4, other arithmetic, place(): return jnp.where(sources >= 0, sources + offset, -1)  2.87 us
  transfers between devices with their start and end apart: 4, of which 2 were waited for; matrix products, arithmetic and copies ran while one was open for 4% of the time, Pallas kernels for 0%

profile of v1, /device:TPU:0, one launch (start us, length us, event | category | flops | bytes accessed | tf_op | source)
XLA Modules:
  0.0 77.8 jit_solution(13798376767757172147)
XLA Ops:
  0.6 0.0 copy-start
  0.6 1.0 %copy.154 = f32[1,165,128]{2,1,0:T(8,128)S(1)} copy(f32[1,165,128]{2,0,1:T(1,128)} %param.11) | data formatting | bytes 168960
  1.6 3.0 %collective-permute-start = (f32[165,128]{1,0:T(8,128)S(1)}, f32[165,128]{1,0:T(8,128)S(1)}, u32[]{:S(2)}, u32[]{:S(2)}) collective-permute-start(f32[165,128]{1,0:T(8,128)S(1)} %bitcast.57), channel_id=1, source_target_pairs={{0,1},{1,0},{2,3},{3,2},{4,5},{5,4},{6,7},{7,6},{8,9},{9,8},{10,11... | collective-permute-start | bytes 253448 | tf_op jit(solution)/shard_map/ppermute | solution.py:185
  4.6 0.7 compare_select_fusion.1
  5.3 0.7 add_select_fusion.1
  6.0 0.8 %add_select_fusion = s32[94,128]{1,0:T(8,128)S(1)} fusion(s32[94,128]{1,0:T(8,128)} %param.15, s32[]{:T(128)S(6)} %sub.16), kind=kLoop, calls=%fused_computation.32 | loop fusion | flops 36096 | bytes 96260 | tf_op jit(solution)/shard_map/jit(_where)/select_n | solution.py:229
  6.8 0.7 compare_select_fusion
  7.5 0.9 %fusion.35 = f32[165,128]{1,0:T(8,128)S(1)} fusion(f32[165,128]{1,0:T(8,128)S(1)} %collective-permute-done, f32[1,165,128]{2,0,1:T(1,128)} %param.11), kind=kLoop, calls=%fused_computation.42 | loop fusion | flops 21120 | bytes 253440 | tf_op jit(solution)/shard_map/add | solution.py:186
  8.4 1.5 %collective-permute-start.1 = (f32[165,128]{1,0:T(8,128)S(1)}, f32[165,128]{1,0:T(8,128)S(1)}, u32[]{:S(2)}, u32[]{:S(2)}) collective-permute-start(f32[165,128]{1,0:T(8,128)S(1)} %fusion.35), channel_id=1, source_target_pairs={{0,2},{2,4},{4,6},{6,8},{8,10},{10,12},{12,14},{14,16},{16,18},{18... | collective-permute-start | bytes 253448 | tf_op jit(solution)/shard_map/ppermute | solution.py:194
  9.9 1.3 %collective-permute-start.2 = (f32[165,128]{1,0:T(8,128)S(1)}, f32[165,128]{1,0:T(8,128)S(1)}, u32[]{:S(2)}, u32[]{:S(2)}) collective-permute-start(f32[165,128]{1,0:T(8,128)S(1)} %fusion.35), channel_id=1, source_target_pairs={{2,0},{4,2},{6,4},{8,6},{10,8},{12,10},{14,12},{16,14},{18,16},{20... | collective-permute-start | bytes 253448 | tf_op jit(solution)/shard_map/ppermute | solution.py:195
  11.2 0.1 copy.99
  11.3 3.4 %collective-permute-done.2 = f32[165,128]{1,0:T(8,128)S(1)} collective-permute-done((f32[165,128]{1,0:T(8,128)S(1)}, f32[165,128]{1,0:T(8,128)S(1)}, u32[]{:S(2)}, u32[]{:S(2)}) %collective-permute-start.2) | collective-permute-done | bytes 84512 | tf_op jit(solution)/shard_map/ppermute | solution.py:195
  14.8 0.2 copy.87
  14.9 1.5 %fusion.16 = f32[165,48]{1,0:T(8,128)S(1)} fusion(f32[8,165,165]{2,0,1:T(8,128)S(1)} %copy-done, f32[165,48,8]{0,2,1:T(8,128)S(1)} %bitcast.53), kind=kOutput, calls=%fused_computation.13 | convolution fusion | flops 125452800 | bytes 1156320 | tf_op jit(solution)/shard_map/oab,bpo->ap/dot_general | solution.py:172
  16.5 0.1 slice.25
  16.6 0.1 copy.91
  16.6 1.4 %fusion.22 = f32[1,2,165]{2,1,0:T(2,128)S(1)} fusion(f32[8,165,165]{2,0,1:T(8,128)S(1)} %copy-done, f32[165,2,8]{0,2,1:T(8,128)S(1)} %bitcast.58), kind=kOutput, calls=%fused_computation.15 | convolution fusion | flops 5227200 | bytes 883080 | tf_op jit(solution)/shard_map/oab,bpo->ap/dot_general | solution.py:172
  18.0 23.3 %all-gather = f32[16,2,165]{2,1,0:T(2,128)S(1)} all-gather(f32[1,2,165]{2,1,0:T(2,128)S(1)} %fusion.22), channel_id=1, replica_groups=mesh['dom'=16,'sub'=2] {'dom'}, dimensions={0}, use_global_device_ids=true | all-gather | bytes 22440 | tf_op jit(solution)/shard_map/all_gather | solution.py:225
  41.4 0.1 copy.94
  41.5 1.4 %fusion.13 = f32[165,4]{1,0:T(8,128)S(1)} fusion(f32[8,165,165]{2,0,1:T(8,128)S(1)} %copy-done, f32[165,4,8]{0,2,1:T(8,128)S(1)} %bitcast.56), kind=kOutput, calls=%fused_computation.12 | convolution fusion | flops 10454400 | bytes 894960 | tf_op jit(solution)/shard_map/oab,bpo->ap/dot_general | solution.py:172
  42.9 0.1 select_maximum_fusion.coarse_ref
  43.0 21.4 %shard_map.122 = f32[168,256]{1,0:T(8,128)S(1)} custom-call(f32[168,384]{1,0:T(8,128)S(1)} %pad.24.fine_ref, f32[168,128]{1,0:T(8,128)S(1)} %select_maximum_fusion.coarse_ref, s32[96,128]{1,0:T(8,128)S(1)} %pad.26.fine_list, s32[96,128]{1,0:T(8,128)S(1)} %pad.27.coarse_list, f32[165,165,94]{2,1,0:T(8,128)} %bitcast.61), custom_call_target="tpu_custom_call" | custom-call | flops 5549064192 | bytes 14450688 | tf_op jit(solution)/shard_map/pallas_call | solution.py:109
  64.4 1.6 %collective-permute-start.3 = (f32[168,256]{1,0:T(8,128)S(1)}, f32[168,256]{1,0:T(8,128)S(1)}, u32[]{:S(2)}, u32[]{:S(2)}) collective-permute-start(f32[168,256]{1,0:T(8,128)S(1)} %shard_map.122), channel_id=1, source_target_pairs={{0,1},{1,0},{2,3},{3,2},{4,5},{5,4},{6,7},{7,6},{8,9},{9,8},{10,11... | collective-permute-start | bytes 516104 | tf_op jit(solution)/shard_map/ppermute | solution.py:185
  66.0 5.1 %collective-permute-done.3 = f32[168,256]{1,0:T(8,128)S(1)} collective-permute-done((f32[168,256]{1,0:T(8,128)S(1)}, f32[168,256]{1,0:T(8,128)S(1)}, u32[]{:S(2)}, u32[]{:S(2)}) %collective-permute-start.3) | collective-permute-done | bytes 172064 | tf_op jit(solution)/shard_map/ppermute | solution.py:185
  71.1 0.2 slice_reduce_fusion
  71.3 0.3 multiply_reduce_fusion
  71.6 1.7 %fusion.19 = f32[165,2,8]{0,1,2:T(2,128)S(1)} fusion(f32[8,165,165]{2,0,1:T(8,128)S(1)} %copy-done.3, f32[168,256]{1,0:T(8,128)S(1)} %add.72, f32[8,165]{0,1:T(8,128)S(1)} %multiply_reduce_fusion, s32[]{:T(128)S(6)} %select_n.40), kind=kOutput, calls=%fused_computation.14 | convolution fusion | flops 5227530 | bytes 1534276 | tf_op jit(solution)/shard_map/oab,bp->apo/dot_general | solution.py:176
  73.3 0.1 copy.103
  73.4 1.6 %fusion.10 = f32[165,16,8]{0,1,2:T(8,128)S(1)} fusion(f32[8,165,165]{2,0,1:T(8,128)S(1)} %copy-done.3, f32[165,16]{1,0:T(8,128)S(1)} %copy.103, f32[168,256]{1,0:T(8,128)S(1)} %add.72), kind=kOutput, calls=%fused_computation.11 | convolution fusion | flops 41820240 | bytes 1608192 | tf_op jit(solution)/shard_map/oab,bp->apo/dot_general | solution.py:176
  75.0 0.1 copy.153
  75.1 0.1 copy.107
  75.2 2.5 %shard_map.123 = f32[1,2048]{1,0:T(1,128)} custom-call(f32[168,128]{1,0:T(8,128)S(1)} %pad.28.local_ref, s32[1,2048]{1,0:T(1,128)S(1)} %bitcast.52, f32[3,2048]{1,0:T(4,128)S(1)} %copy-done.2, s32[168,128]{1,0:T(8,128)S(1)} %copy-done.1), custom_call_target="tpu_custom_call" | custom-call | tf_op jit(solution)/shard_map/pallas_call | solution.py:162
  (24 shorter events, 0.2 us)
Async XLA Ops:
  0.6 14.3 %copy-start = (f32[8,165,165]{2,0,1:T(8,128)S(1)}, f32[8,165,165]{2,0,1:T(8,128)}, u32[]{:S(2)}) copy-start(f32[8,165,165]{2,0,1:T(8,128)} %param.12) | copy-start | bytes 2613604
  1.6 5.8 %collective-permute-start = (f32[165,128]{1,0:T(8,128)S(1)}, f32[165,128]{1,0:T(8,128)S(1)}, u32[]{:S(2)}, u32[]{:S(2)}) collective-permute-start(f32[165,128]{1,0:T(8,128)S(1)} %bitcast.57), channel_id=1, source_target_pairs={{0,1},{1,0},{2,3},{3,2},{4,5},{5,4},{6,7},{7,6},{8,9},{9,8},{10,11... | collective-permute-start | bytes 253448 | tf_op jit(solution)/shard_map/ppermute | solution.py:185
  8.4 2.9 %collective-permute-start.1 = (f32[165,128]{1,0:T(8,128)S(1)}, f32[165,128]{1,0:T(8,128)S(1)}, u32[]{:S(2)}, u32[]{:S(2)}) collective-permute-start(f32[165,128]{1,0:T(8,128)S(1)} %fusion.35), channel_id=1, source_target_pairs={{0,2},{2,4},{4,6},{6,8},{8,10},{10,12},{12,14},{14,16},{16,18},{18... | collective-permute-start | bytes 253448 | tf_op jit(solution)/shard_map/ppermute | solution.py:194
  9.9 4.9 %collective-permute-start.2 = (f32[165,128]{1,0:T(8,128)S(1)}, f32[165,128]{1,0:T(8,128)S(1)}, u32[]{:S(2)}, u32[]{:S(2)}) collective-permute-start(f32[165,128]{1,0:T(8,128)S(1)} %fusion.35), channel_id=1, source_target_pairs={{2,0},{4,2},{6,4},{8,6},{10,8},{12,10},{14,12},{16,14},{18,16},{20... | collective-permute-start | bytes 253448 | tf_op jit(solution)/shard_map/ppermute | solution.py:195
  43.0 23.0 %copy-start.5 = (s32[2048]{0:T(1024)S(1)}, s32[2048]{0:T(1024)}, u32[]{:S(2)}) copy-start(s32[2048]{0:T(1024)} %param.20) | copy-start | bytes 24580
  43.0 28.3 %copy-start.3 = (f32[8,165,165]{2,0,1:T(8,128)S(1)}, f32[8,165,165]{2,0,1:T(8,128)}, u32[]{:S(2)}) copy-start(f32[8,165,165]{2,0,1:T(8,128)} %param.14) | copy-start | bytes 2613604
  64.4 6.7 %collective-permute-start.3 = (f32[168,256]{1,0:T(8,128)S(1)}, f32[168,256]{1,0:T(8,128)S(1)}, u32[]{:S(2)}, u32[]{:S(2)}) collective-permute-start(f32[168,256]{1,0:T(8,128)S(1)} %shard_map.122), channel_id=1, source_target_pairs={{0,1},{1,0},{2,3},{3,2},{4,5},{5,4},{6,7},{7,6},{8,9},{9,8},{10,11... | collective-permute-start | bytes 516104 | tf_op jit(solution)/shard_map/ppermute | solution.py:185
  73.2 2.0 %copy-start.1 = (s32[168,128]{1,0:T(8,128)S(1)}, s32[168,128]{1,0:T(8,128)}, u32[]{:S(2)}) copy-start(s32[168,128]{1,0:T(8,128)} %constant.70.exponent_ref) | copy-start | bytes 258052
  73.2 2.0 %copy-start.2 = (f32[3,2048]{1,0:T(4,128)S(1)}, f32[3,2048]{1,0:T(4,128)}, u32[]{:S(2)}) copy-start(f32[3,2048]{1,0:T(4,128)} %position_ref.1) | copy-start | bytes 73732
  75.2 2.6 %copy-start.4 = (f32[165,128]{1,0:T(8,128)}, f32[165,128]{1,0:T(8,128)S(1)}, u32[]{:S(2)}) copy-start(f32[165,128]{1,0:T(8,128)S(1)} %slice_add_fusion.2) | copy-start | bytes 253444

commit v2 on v1

--- a/solution.py
+++ b/solution.py
@@ -166,6 +166,98 @@
     )(local, leaves[None], positions, table)[0]
 
 
+def exchange_kernel(
+    domains, subs, block_ref, top_ref, low_out, high_out, tops_out,
+    low, high, tops, side_send, side_recv, top_send, top_recv, own_sem,
+):
+    domain, sub = lax.axis_index("dom"), lax.axis_index("sub")
+    count = domains * subs
+    flat = domain * subs + sub
+    mesh = pl.DeviceIdType.MESH
+
+    def peer(offset):
+        place = lax.rem(flat + offset, count)
+        return {"dom": place // subs, "sub": lax.rem(place, subs)}
+
+    barrier = pltpu.get_barrier_semaphore()
+
+    def greet(offset, carry):
+        pl.semaphore_signal(barrier, inc=1, device_id=peer(offset), device_id_type=mesh)
+        return carry
+
+    lax.fori_loop(1, count, greet, 0)
+    own = pltpu.make_async_copy(top_ref, tops.at[count - 1], own_sem)
+    own.start()
+    pl.semaphore_wait(barrier, count - 1)
+
+    def send(offset, carry):
+        pltpu.make_async_remote_copy(
+            src_ref=top_ref,
+            dst_ref=tops.at[offset - 1],
+            send_sem=top_send,
+            recv_sem=top_recv,
+            device_id=peer(offset),
+            device_id_type=mesh,
+        ).start()
+        return carry
+
+    sides = []
+    for index, (target, move) in enumerate(((low, 1), (high, domains - 1))):
+        side = pltpu.make_async_remote_copy(
+            src_ref=block_ref,
+            dst_ref=target,
+            send_sem=side_send.at[index],
+            recv_sem=side_recv.at[index],
+            device_id={"dom": lax.rem(domain + move, domains), "sub": sub},
+            device_id_type=mesh,
+        )
+        side.start()
+        sides.append(side)
+    lax.fori_loop(1, count, send, 0)
+    own.wait()
+    arrived = tops.at[pl.ds(0, count - 1)]
+    pltpu.make_async_copy(arrived, arrived, top_recv).wait()
+    tops_out[...] = jnp.zeros_like(tops_out)
+
+    def gather(offset, carry):
+        source = lax.rem(flat + count - offset, count) // subs
+        tops_out[source] = tops_out[source] + tops[lax.rem(offset + count - 1, count)]
+        return carry
+
+    lax.fori_loop(0, count, gather, 0)
+    for side in sides:
+        side.wait()
+    low_out[...] = low[...]
+    high_out[...] = high[...]
+    pltpu.make_async_copy(arrived, arrived, top_send).wait()
+
+
+def exchange(block, top_rows):
+    domains, subs = lax.axis_size("dom"), lax.axis_size("sub")
+    vmem = pl.BlockSpec(memory_space=pltpu.VMEM)
+    return pl.pallas_call(
+        functools.partial(exchange_kernel, domains, subs),
+        in_specs=[vmem, vmem],
+        out_specs=[vmem] * 3,
+        out_shape=[
+            jax.ShapeDtypeStruct(block.shape, jnp.float32),
+            jax.ShapeDtypeStruct(block.shape, jnp.float32),
+            jax.ShapeDtypeStruct((domains,) + top_rows.shape, jnp.float32),
+        ],
+        scratch_shapes=[
+            pltpu.VMEM(block.shape, jnp.float32),
+            pltpu.VMEM(block.shape, jnp.float32),
+            pltpu.VMEM((domains * subs,) + top_rows.shape, jnp.float32),
+            pltpu.SemaphoreType.DMA((2,)),
+            pltpu.SemaphoreType.DMA((2,)),
+            pltpu.SemaphoreType.DMA,
+            pltpu.SemaphoreType.DMA,
+            pltpu.SemaphoreType.DMA,
+        ],
+        compiler_params=pltpu.CompilerParams(collective_id=0, has_side_effects=True),
+    )(block, top_rows)
+
+
 def upward(moments, upward_ops):
     parents = moments.shape[1] // 8
     grouped = moments.reshape(moments.shape[0], parents, 8)
@@ -185,15 +277,6 @@
         moving = lax.ppermute(moving, "sub", ring)
         total = total + moving
     return total
-
-
-def extended(block):
-    count = lax.axis_size("dom")
-    forward = [(i, i + 1) for i in range(count - 1)]
-    backward = [(target, source) for source, target in forward]
-    low = lax.ppermute(block, "dom", forward)
-    high = lax.ppermute(block, "dom", backward)
-    return jnp.concatenate([low, block, high], axis=1)
 
 
 def shards(
@@ -219,10 +302,14 @@
     upper_first = domain * top_cells // 8
     upper_sources = lax.dynamic_slice_in_dim(upper_list, upper_first, upper_span, 1)
 
-    wide_fine = extended(settle(fine_partial[0]))
-    wide_mid = upward(wide_fine, upward_ops)
-    own_top = upward(wide_mid[:, mid_cells : 2 * mid_cells], upward_ops)
-    top_moments = lax.all_gather(own_top, "dom", axis=1, tiled=True)
+    partial = fine_partial[0]
+    own_top = upward(upward(partial, upward_ops), upward_ops)
+    top_rows = jnp.pad(jnp.transpose(own_top), ((0, 0), (0, 2 * LANES - coeffs)))
+    block = jnp.pad(settle(partial), ((0, rows - coeffs), (0, 0)))
+    low, high, tops = exchange(block, top_rows)
+    wide_fine = jnp.concatenate([low, block, high], axis=1)
+    wide_mid = upward(wide_fine[:coeffs], upward_ops)
+    top_moments = jnp.transpose(tops.reshape(-1, 2 * LANES)[:, :coeffs])
     upper_moments = upward(top_moments, upward_ops)
 
     def place(sources, offset):
@@ -247,7 +334,7 @@
     )
     fine_sources = place(fine_list, slab_cells - domain * slab_cells)
     terms = interact(
-        padded(wide_fine, rows, wide_fine.shape[1], 0),
+        wide_fine,
         padded(coarse, rows, round_up(coarse.shape[1], LANES), 0),
         padded(fine_sources, depth, LANES, -1),
         padded(coarse_sources, depth, LANES, -1),

time: 78.3 us -> 64.5 us (0.82)
  blocking collectives: 23.3 us -> 0 us
  Pallas kernels: 23.9 us -> 34.9 us
  waiting for transfers between devices: 8.54 us -> 5.15 us
  starting transfers between devices: 7.28 us -> 4.19 us
  matrix products: 7.56 us -> 10.4 us
  local copies, waits for them, and re-layouts: 2.09 us -> 4.17 us
    all_gather x1 -> x0, blocking collectives: 23.3 us -> none  [shards(): top_moments = lax.all_gather(own_top, 'dom', axis=1, tiled=True)]
    pallas_call x0 -> x1, Pallas kernels: none -> 11 us  [exchange(): pl.pallas_call(functools.partial(exchange_kernel, domains, subs), in_spec...]
    ppermute x2 -> x0, waiting for transfers between devices: 3.41 us -> none  [the longest x1 3.41 us: extended(): high = lax.ppermute(block, 'dom', backward)]
    dot_general x3 -> x4, matrix products: 4.3 us -> 7.1 us  [upward(): return jnp.einsum('oab,bpo->ap', upward_ops, grouped, precision=precise)]
    ppermute x2 -> x0, starting transfers between devices: 2.76 us -> none  [the longest x1 1.46 us: extended(): low = lax.ppermute(block, 'dom', forward)]
    pad x0 -> x2, local copies, waits for them, and re-layouts: none -> 1.25 us  [the longest x1 0.64 us: shards(): block = jnp.pad(settle(partial), ((0, rows - coeffs), (0, 0)))]
    unnamed x15 -> x19, local copies, waits for them, and re-layouts: 1.17 us -> 2.14 us
    concatenate x1, other arithmetic: 0.02 us -> 0.99 us  [shards(): wide_fine = jnp.concatenate([low, block, high], axis=1)]
  transfers between devices with their start and end apart: 4 -> 2, of which waited for: 2 -> 1; matrix products, arithmetic and copies ran while one was open for 4% -> 14% of each run, Pallas kernels for 0% -> 0%
where the time goes in v2:
time: 64.5 us; the launch traced here: 63.9 us
  Pallas kernels  34.9 us (54%)
  matrix products  10.4 us (16%)
  waiting for transfers between devices  5.15 us (8%)
  other arithmetic  4.3 us (7%)
  starting transfers between devices  4.19 us (6%)
  local copies, waits for them, and re-layouts  4.17 us (6%)
  between operations  0.89 us (1%)
    pallas_call x1, Pallas kernels, interact(): pl.pallas_call(functools.partial(interact_kernel, coeffs, slots, group),...  21.4 us
    pallas_call x1, Pallas kernels, exchange(): pl.pallas_call(functools.partial(exchange_kernel, domains, subs), in_spec...  11 us
    dot_general x4, matrix products, upward(): return jnp.einsum('oab,bpo->ap', upward_ops, grouped, precision=precise)  7.1 us
    ppermute x2, waiting for transfers between devices, settle(): moving = lax.ppermute(moving, 'sub', ring)  5.15 us
    ppermute x2, starting transfers between devices, settle(): moving = lax.ppermute(moving, 'sub', ring)  4.19 us
    dot_general x2, matrix products, downward(): jnp.einsum('oab,bp->apo', downward_ops, expansions, precision=precise)  3.26 us
    select_n x4, other arithmetic, place(): return jnp.where(sources >= 0, sources + offset, -1)  2.88 us
    pallas_call x1, Pallas kernels, evaluate(): pl.pallas_call(potential_kernel, out_shape=jax.ShapeDtypeStruct((1, leave...  2.54 us
  transfers between devices with their start and end apart: 2, of which 1 were waited for; matrix products, arithmetic and copies ran while one was open for 14% of the time, Pallas kernels for 0%

profile of v2, /device:TPU:0, one launch (start us, length us, event | category | flops | bytes accessed | tf_op | source)
XLA Modules:
  0.0 63.9 jit_solution(12768096629432329587)
XLA Ops:
  0.6 1.0 %copy.167 = f32[1,165,128]{2,1,0:T(8,128)S(1)} copy(f32[1,165,128]{2,0,1:T(1,128)} %param.11) | data formatting | bytes 168960
  1.6 3.0 %collective-permute-start = (f32[165,128]{1,0:T(8,128)S(1)}, f32[165,128]{1,0:T(8,128)S(1)}, u32[]{:S(2)}, u32[]{:S(2)}) collective-permute-start(f32[165,128]{1,0:T(8,128)S(1)} %bitcast.73), channel_id=1, source_target_pairs={{0,1},{1,0},{2,3},{3,2},{4,5},{5,4},{6,7},{7,6},{8,9},{9,8},{10,11... | collective-permute-start | bytes 253448 | tf_op jit(solution)/shard_map/ppermute | solution.py:277
  4.6 1.0 %copy.87 = f32[1,165,128]{1,2,0:T(8,128)S(1)} copy(f32[1,165,128]{2,0,1:T(1,128)} %param.11) | data formatting | bytes 168960 | tf_op args[0]
  5.6 0.7 %compare_select_fusion.1 = s32[94,2]{0,1:T(2,128)S(1)} fusion(s32[94,2]{0,1:T(2,128)} %param.17), kind=kLoop, calls=%fused_computation.45 | loop fusion | flops 564 | bytes 1504 | tf_op jit(solution)/shard_map/jit(_where)/select_n | solution.py:316
  6.3 0.7 %compare_select_fusion = s32[94,1]{0,1:T(1,128)S(1)} fusion(s32[94,4]{0,1:T(4,128)} %param.18, s32[]{:T(128)S(6)} %select_n.37), kind=kLoop, calls=%fused_computation.44 | loop fusion | flops 282 | bytes 756 | tf_op jit(solution)/shard_map/jit(_where)/select_n | solution.py:316
  7.0 0.7 %add_select_fusion.1 = s32[94,16]{0,1:T(8,128)S(1)} fusion(s32[94,16]{0,1:T(8,128)} %param.16, s32[]{:T(128)S(6)} %sub.17), kind=kLoop, calls=%fused_computation.42 | loop fusion | flops 4512 | bytes 12036 | tf_op jit(solution)/shard_map/jit(_where)/select_n | solution.py:316
  7.7 0.1 copy.101
  7.8 0.8 %add_select_fusion = s32[94,128]{1,0:T(8,128)S(1)} fusion(s32[94,128]{1,0:T(8,128)} %param.15, s32[]{:T(128)S(6)} %sub.16), kind=kLoop, calls=%fused_computation.37 | loop fusion | flops 36096 | bytes 96260 | tf_op jit(solution)/shard_map/jit(_where)/select_n | solution.py:316
  8.7 2.8 %fusion.25 = f32[165,2,8]{0,2,1:T(8,128)S(1)} fusion(f32[8,165,165]{2,0,1:T(8,128)} %param.12, f32[2,8,165,8]{2,3,1,0:T(8,128)S(1)} %bitcast.70), kind=kOutput, calls=%fused_computation.18 | convolution fusion | flops 41817600 | bytes 966240 | tf_op jit(solution)/shard_map/oab,bpo->ap/dot_general | solution.py:264
  11.5 0.0 copy-done.2
  11.5 1.4 %fusion.28 = f32[2,165]{1,0:T(2,128)S(1)} fusion(f32[8,165,165]{2,0,1:T(8,128)S(1)} %copy-done.2, f32[165,2,8]{0,2,1:T(8,128)S(1)} %fusion.25), kind=kOutput, calls=%fused_computation.19 | convolution fusion | flops 5227200 | bytes 883080 | tf_op jit(solution)/shard_map/oab,bpo->ap/dot_general | solution.py:264
  12.9 0.6 pad.28.top_ref
  13.5 0.6 %pad.27.block_ref = f32[168,128]{1,0:T(8,128)} pad(f32[165,128]{1,0:T(8,128)S(1)} %fusion.42, f32[]{:T(128)} %constant.40.clone.1), padding=0_3x0_0 | pad | bytes 170500 | tf_op jit(solution)/shard_map/jit(_pad)/pad | solution.py:308
  14.1 11.0 %shard_map.122 = (f32[168,128]{1,0:T(8,128)}, f32[168,128]{1,0:T(8,128)}, f32[16,2,256]{2,1,0:T(2,128)}) custom-call(f32[168,128]{1,0:T(8,128)} %pad.27.block_ref, f32[2,256]{1,0:T(2,128)} %pad.28.top_ref), custom_call_target="tpu_custom_call" | custom-call | tf_op jit(solution)/shard_map/pallas_call | solution.py:238
  25.1 1.0 %pad_maximum_fusion.fine_ref = f32[168,384]{1,0:T(8,128)S(1)} fusion(f32[168,128]{1,0:T(8,128)} %get-tuple-element.6, f32[168,128]{1,0:T(8,128)} %pad.27.block_ref, f32[168,128]{1,0:T(8,128)} %get-tuple-element.5), kind=kLoop, calls=%fused_computation.21 | loop fusion | flops 129024 | bytes 516096 | tf_op jit(solution)/shard_map/concatenate | solution.py:310
  26.1 0.2 copy.92
  26.3 1.5 %fusion.19 = f32[165,48]{1,0:T(8,128)S(1)} fusion(f32[8,165,165]{2,0,1:T(8,128)S(1)} %copy-done.2, f32[165,48,8]{0,2,1:T(8,128)S(1)} %bitcast.69), kind=kOutput, calls=%fused_computation.16 | convolution fusion | flops 125452800 | bytes 1156320 | tf_op jit(solution)/shard_map/oab,bpo->ap/dot_general | solution.py:264
  27.9 0.1 copy.124
  28.0 1.4 %fusion.16 = f32[165,4]{1,0:T(8,128)S(1)} fusion(f32[8,165,165]{2,0,1:T(8,128)S(1)} %copy-done.2, f32[165,4,8]{0,2,1:T(8,128)S(1)} %get-tuple-element.9), kind=kOutput, calls=%fused_computation.15 | convolution fusion | flops 10454400 | bytes 894960 | tf_op jit(solution)/shard_map/oab,bpo->ap/dot_general | solution.py:264
  29.4 0.1 select_maximum_fusion.coarse_ref
  29.5 21.4 %shard_map.123 = f32[168,256]{1,0:T(8,128)S(1)} custom-call(f32[168,384]{1,0:T(8,128)S(1)} %pad_maximum_fusion.fine_ref, f32[168,128]{1,0:T(8,128)S(1)} %select_maximum_fusion.coarse_ref, s32[96,128]{1,0:T(8,128)S(1)} %pad.30.fine_list, s32[96,128]{1,0:T(8,128)S(1)} %pad.31.coarse_list, f32[165,165,94]{2,1,0:T(8,128)} %bitcast.76), custom_call_target="tpu_custom_call" | custom-call | flops 5549064192 | bytes 14450688 | tf_op jit(solution)/shard_map/pallas_call | solution.py:109
  50.9 1.2 %collective-permute-start.1 = (f32[168,256]{1,0:T(8,128)S(1)}, f32[168,256]{1,0:T(8,128)S(1)}, u32[]{:S(2)}, u32[]{:S(2)}) collective-permute-start(f32[168,256]{1,0:T(8,128)S(1)} %shard_map.123), channel_id=1, source_target_pairs={{0,1},{1,0},{2,3},{3,2},{4,5},{5,4},{6,7},{7,6},{8,9},{9,8},{10,11... | collective-permute-start | bytes 516104 | tf_op jit(solution)/shard_map/ppermute | solution.py:277
  52.1 5.1 %collective-permute-done.1 = f32[168,256]{1,0:T(8,128)S(1)} collective-permute-done((f32[168,256]{1,0:T(8,128)S(1)}, f32[168,256]{1,0:T(8,128)S(1)}, u32[]{:S(2)}, u32[]{:S(2)}) %collective-permute-start.1) | collective-permute-done | bytes 172064 | tf_op jit(solution)/shard_map/ppermute | solution.py:277
  57.3 0.2 slice_reduce_fusion
  57.5 0.3 multiply_reduce_fusion
  57.7 1.7 %fusion.22 = f32[165,2,8]{0,1,2:T(2,128)S(1)} fusion(f32[8,165,165]{2,0,1:T(8,128)S(1)} %copy-done.3, f32[168,256]{1,0:T(8,128)S(1)} %add.74, f32[8,165]{0,1:T(8,128)S(1)} %multiply_reduce_fusion, s32[]{:T(128)S(6)} %select_n.40), kind=kOutput, calls=%fused_computation.17 | convolution fusion | flops 5227530 | bytes 1534276 | tf_op jit(solution)/shard_map/oab,bp->apo/dot_general | solution.py:268
  59.4 0.0 copy-start
  59.4 0.1 copy.105
  59.5 1.6 %fusion.13 = f32[165,16,8]{0,1,2:T(8,128)S(1)} fusion(f32[8,165,165]{2,0,1:T(8,128)S(1)} %copy-done.3, f32[165,16]{1,0:T(8,128)S(1)} %copy.105, f32[168,256]{1,0:T(8,128)S(1)} %add.74), kind=kOutput, calls=%fused_computation.14 | convolution fusion | flops 41820240 | bytes 1608192 | tf_op jit(solution)/shard_map/oab,bp->apo/dot_general | solution.py:268
  61.1 0.1 copy.166
  61.2 0.1 copy.109
  61.4 2.5 %shard_map.124 = f32[1,2048]{1,0:T(1,128)} custom-call(f32[168,128]{1,0:T(8,128)S(1)} %pad.32.local_ref, s32[1,2048]{1,0:T(1,128)S(1)} %bitcast.68, f32[3,2048]{1,0:T(4,128)S(1)} %copy-done.1, s32[168,128]{1,0:T(8,128)S(1)} %copy-done), custom_call_target="tpu_custom_call" | custom-call | tf_op jit(solution)/shard_map/pallas_call | solution.py:162
  (26 shorter events, 0.2 us)
Async XLA Ops:
  0.6 10.9 %copy-start.2 = (f32[8,165,165]{2,0,1:T(8,128)S(1)}, f32[8,165,165]{2,0,1:T(8,128)}, u32[]{:S(2)}) copy-start(f32[8,165,165]{2,0,1:T(8,128)} %param.12) | copy-start | bytes 2613604
  1.6 11.8 %collective-permute-start = (f32[165,128]{1,0:T(8,128)S(1)}, f32[165,128]{1,0:T(8,128)S(1)}, u32[]{:S(2)}, u32[]{:S(2)}) collective-permute-start(f32[165,128]{1,0:T(8,128)S(1)} %bitcast.73), channel_id=1, source_target_pairs={{0,1},{1,0},{2,3},{3,2},{4,5},{5,4},{6,7},{7,6},{8,9},{9,8},{10,11... | collective-permute-start | bytes 253448 | tf_op jit(solution)/shard_map/ppermute | solution.py:277
  8.7 4.8 %copy-start.4 = (f32[1,165,128]{2,0,1:T(1,128)S(1)}, f32[1,165,128]{2,0,1:T(1,128)}, u32[]{:S(2)}) copy-start(f32[1,165,128]{2,0,1:T(1,128)} %param.11) | copy-start | bytes 253444
  26.1 1.7 %copy-start.6 = (f32[16,2,256]{2,1,0:T(2,128)S(1)}, f32[16,2,256]{2,1,0:T(2,128)}, u32[]{:S(2)}) copy-start(f32[16,2,256]{2,1,0:T(2,128)} %get-tuple-element.7) | copy-start | bytes 98308
  29.5 22.6 %copy-start.7 = (s32[2048]{0:T(1024)S(1)}, s32[2048]{0:T(1024)}, u32[]{:S(2)}) copy-start(s32[2048]{0:T(1024)} %param.20) | copy-start | bytes 24580
  29.5 28.0 %copy-start.3 = (f32[8,165,165]{2,0,1:T(8,128)S(1)}, f32[8,165,165]{2,0,1:T(8,128)}, u32[]{:S(2)}) copy-start(f32[8,165,165]{2,0,1:T(8,128)} %param.14) | copy-start | bytes 2613604
  50.9 6.4 %collective-permute-start.1 = (f32[168,256]{1,0:T(8,128)S(1)}, f32[168,256]{1,0:T(8,128)S(1)}, u32[]{:S(2)}, u32[]{:S(2)}) collective-permute-start(f32[168,256]{1,0:T(8,128)S(1)} %shard_map.123), channel_id=1, source_target_pairs={{0,1},{1,0},{2,3},{3,2},{4,5},{5,4},{6,7},{7,6},{8,9},{9,8},{10,11... | collective-permute-start | bytes 516104 | tf_op jit(solution)/shard_map/ppermute | solution.py:277
  59.4 2.0 %copy-start = (s32[168,128]{1,0:T(8,128)S(1)}, s32[168,128]{1,0:T(8,128)}, u32[]{:S(2)}) copy-start(s32[168,128]{1,0:T(8,128)} %constant.72.exponent_ref) | copy-start | bytes 258052
  59.4 2.0 %copy-start.1 = (f32[3,2048]{1,0:T(4,128)S(1)}, f32[3,2048]{1,0:T(4,128)}, u32[]{:S(2)}) copy-start(f32[3,2048]{1,0:T(4,128)} %position_ref.1) | copy-start | bytes 73732
  61.3 2.6 %copy-start.5 = (f32[165,128]{1,0:T(8,128)}, f32[165,128]{1,0:T(8,128)S(1)}, u32[]{:S(2)}) copy-start(f32[165,128]{1,0:T(8,128)S(1)} %slice_add_fusion.2) | copy-start | bytes 253444

commit v3 on v2

--- a/solution.py
+++ b/solution.py
@@ -39,8 +39,9 @@
 
 
 def interact_kernel(
-    coeffs, slots, group, fine_ref, coarse_ref, fine_list, coarse_list, ops_ref, out_ref,
-    fine_table, coarse_table, fine_picked, coarse_picked,
+    coeffs, slots, group, spread, tops, fine_ref, tops_ref, upward_ref, fine_list, coarse_list,
+    ops_ref, out_ref,
+    fine_table, coarse_table, fine_picked, coarse_picked, held,
 ):
     rows = fine_ref.shape[0]
     depth = fine_list.shape[0]
@@ -48,8 +49,22 @@
 
     @pl.when(step == 0)
     def _():
-        for source, table in ((fine_ref, fine_table), (coarse_ref, coarse_table)):
-            high, low = halves(source[...])
+        ops_high, ops_low = split_upward(upward_ref, held)
+        width = coarse_table.shape[1]
+
+        def shifted(value, amount):
+            extra = width - value.shape[1]
+            if extra:
+                filler = jnp.zeros((rows, extra), jnp.float32)
+                value = jnp.concatenate([value, filler], axis=1)
+            return pltpu.roll(value, amount, 1) if amount else value
+
+        top_moments = jnp.transpose(tops_ref[...])[:rows]
+        coarse = shifted(raise_level(fine_ref[...], ops_high, ops_low), 0)
+        coarse += shifted(top_moments, spread)
+        coarse += shifted(raise_level(top_moments, ops_high, ops_low), spread + tops)
+        for source, table in ((fine_ref[...], fine_table), (coarse, coarse_table)):
+            high, low = halves(source)
             table[...] = jnp.concatenate([high, low], axis=0)
 
         def pick(batch, carry):
@@ -99,19 +114,19 @@
         )
 
 
-def interact(fine, coarse, fine_list, coarse_list, ops):
+def interact(fine, tops_rows, upward_ops, fine_list, coarse_list, ops, spread, tops, coarse_width):
     coeffs, _, slots = ops.shape
     rows, width = fine.shape
-    coarse_width = coarse.shape[1]
     depth = fine_list.shape[0]
     group = 24
     whole = lambda array: pl.BlockSpec(array.shape, lambda i: (0, 0))
     return pl.pallas_call(
-        functools.partial(interact_kernel, coeffs, slots, group),
+        functools.partial(interact_kernel, coeffs, slots, group, spread, tops),
         grid=(rows // group,),
         in_specs=[
             whole(fine),
-            whole(coarse),
+            whole(tops_rows),
+            pl.BlockSpec((coeffs, 8, coeffs), lambda i: (0, 0, 0)),
             whole(fine_list),
             whole(coarse_list),
             pl.BlockSpec((rows, group, LANES), lambda i: (0, i, 0)),
@@ -123,6 +138,7 @@
             pltpu.VMEM((2 * rows, coarse_width), jnp.bfloat16),
             pltpu.VMEM((rows, depth, LANES), jnp.float32),
             pltpu.VMEM((rows, depth, LANES), jnp.float32),
+            pltpu.VMEM((rows, 8, 2 * LANES), jnp.float32),
         ],
         compiler_params=pltpu.CompilerParams(vmem_limit_bytes=48 * 1024 * 1024),
         cost_estimate=pl.CostEstimate(
@@ -130,7 +146,7 @@
             bytes_accessed=4 * rows * rows * LANES,
             transcendentals=0,
         ),
-    )(fine, coarse, fine_list, coarse_list, ops)
+    )(fine, tops_rows, jnp.transpose(upward_ops, (1, 0, 2)), fine_list, coarse_list, ops)
 
 
 def potential_kernel(local_ref, leaf_ref, position_ref, exponent_ref, out_ref):
@@ -166,14 +182,81 @@
     )(local, leaves[None], positions, table)[0]
 
 
+def raise_level(moments, ops_high, ops_low):
+    rows, width = moments.shape
+    parents = round_up(width // 8, LANES)
+    high, low = halves(moments)
+    source = lax.broadcasted_iota(jnp.int32, (width, 8 * parents), 0)
+    target = lax.broadcasted_iota(jnp.int32, (width, 8 * parents), 1)
+    wanted = 8 * (target % parents) + target // parents
+    chosen = jnp.where(source == wanted, 1.0, 0.0).astype(jnp.bfloat16)
+    both = jnp.dot(
+        jnp.concatenate([high, low], axis=0), chosen, preferred_element_type=jnp.float32
+    )
+    filler = jnp.zeros((2 * LANES - rows, parents), jnp.float32)
+    stacks = []
+    for first in (0, rows):
+        pieces = []
+        for o in range(8):
+            pieces += [both[first : first + rows, o * parents : (o + 1) * parents], filler]
+        stacks.append(jnp.concatenate(pieces, axis=0).astype(jnp.bfloat16))
+    dot = functools.partial(jnp.dot, preferred_element_type=jnp.float32)
+    return dot(ops_high, stacks[0]) + dot(ops_high, stacks[1]) + dot(ops_low, stacks[0])
+
+
+def split_upward(upward_ref, held):
+    coeffs = upward_ref.shape[0]
+    held[...] = jnp.zeros_like(held)
+    held[:coeffs, :, :coeffs] = upward_ref[...]
+    ops = jnp.swapaxes(held[...], 0, 1)
+    return halves(jnp.concatenate([ops[o] for o in range(8)], axis=1))
+
+
+def prepare_kernel(
+    counts, partial_ref, upward_ref, fine_ref, mid_ref, top_ref, upper_ref,
+    block_out, rows_out, fine_out, coarse_out, held, lists,
+):
+    rows = block_out.shape[0]
+    coeffs = partial_ref.shape[0]
+    slots = fine_ref.shape[0]
+    slab, mid, top, spread, tops = counts
+    domain = lax.axis_index("dom")
+    block_out[...] = jnp.zeros_like(block_out)
+    block_out[:coeffs, :] = partial_ref[...]
+    high, low = split_upward(upward_ref, held)
+    top_moments = raise_level(raise_level(block_out[...], high, low), high, low)
+    filler = jnp.zeros((2 * LANES - rows, LANES), jnp.float32)
+    turned = jnp.transpose(jnp.concatenate([top_moments, filler], axis=0))
+    rows_out[...] = turned[: rows_out.shape[0]]
+
+    def place(sources, offset):
+        return jnp.where(sources >= 0, sources + offset, -1)
+
+    fine_out[...] = jnp.full_like(fine_out, -1)
+    fine_out[:slots, :] = place(fine_ref[...], slab - domain * slab)
+    lists[...] = jnp.full_like(lists, -1.0)
+    start = 0
+    for part in (
+        place(mid_ref[...], mid - domain * mid),
+        place(top_ref[...], spread),
+        place(upper_ref[pl.ds(domain * top // 8, 1), :], spread + tops),
+    ):
+        lists[start : start + part.shape[0], :slots] = part.astype(jnp.float32)
+        start += part.shape[0]
+    coarse = jnp.transpose(lists[...])
+    coarse_out[...] = coarse[: coarse_out.shape[0]].astype(jnp.int32)
+
+
 def exchange_kernel(
-    domains, subs, block_ref, top_ref, low_out, high_out, tops_out,
-    low, high, tops, side_send, side_recv, top_send, top_recv, own_sem,
+    domains, subs, block_ref, top_ref, wide_out, tops_out,
+    sides, tops, side_send, side_recv, top_send, top_recv, own_sem,
 ):
     domain, sub = lax.axis_index("dom"), lax.axis_index("sub")
     count = domains * subs
     flat = domain * subs + sub
     mesh = pl.DeviceIdType.MESH
+    cells = block_ref.shape[1]
+    top_cells = top_ref.shape[0]
 
     def peer(offset):
         place = lax.rem(flat + offset, count)
@@ -189,6 +272,24 @@
     own = pltpu.make_async_copy(top_ref, tops.at[count - 1], own_sem)
     own.start()
     pl.semaphore_wait(barrier, count - 1)
+    copies = []
+    for turn in range(subs):
+        for index, move in enumerate((1, domains - 1, 0)):
+            if turn == 0 and move == 0:
+                continue
+            side = pltpu.make_async_remote_copy(
+                src_ref=block_ref,
+                dst_ref=sides.at[index, turn],
+                send_sem=side_send.at[index, turn],
+                recv_sem=side_recv.at[index, turn],
+                device_id={
+                    "dom": lax.rem(domain + move, domains),
+                    "sub": lax.rem(sub + turn, subs),
+                },
+                device_id_type=mesh,
+            )
+            side.start()
+            copies.append(side)
 
     def send(offset, carry):
         pltpu.make_async_remote_copy(
@@ -201,18 +302,6 @@
         ).start()
         return carry
 
-    sides = []
-    for index, (target, move) in enumerate(((low, 1), (high, domains - 1))):
-        side = pltpu.make_async_remote_copy(
-            src_ref=block_ref,
-            dst_ref=target,
-            send_sem=side_send.at[index],
-            recv_sem=side_recv.at[index],
-            device_id={"dom": lax.rem(domain + move, domains), "sub": sub},
-            device_id_type=mesh,
-        )
-        side.start()
-        sides.append(side)
     lax.fori_loop(1, count, send, 0)
     own.wait()
     arrived = tops.at[pl.ds(0, count - 1)]
@@ -221,35 +310,40 @@
 
     def gather(offset, carry):
         source = lax.rem(flat + count - offset, count) // subs
-        tops_out[source] = tops_out[source] + tops[lax.rem(offset + count - 1, count)]
+        slot = lax.rem(offset + count - 1, count)
+        for r in range(top_cells):
+            at = pl.ds(source * top_cells + r, 1)
+            tops_out[at, :] = tops_out[at, :] + tops[slot, r : r + 1, :]
         return carry
 
     lax.fori_loop(0, count, gather, 0)
-    for side in sides:
+    for side in copies:
         side.wait()
-    low_out[...] = low[...]
-    high_out[...] = high[...]
+    for index, start in ((0, 0), (2, cells), (1, 2 * cells)):
+        held = [block_ref[...]] if index == 2 else [sides[index, 0]]
+        for turn in range(1, subs):
+            held.append(sides[index, turn])
+        wide_out[:, start : start + cells] = sum(held[1:], held[0])
     pltpu.make_async_copy(arrived, arrived, top_send).wait()
 
 
-def exchange(block, top_rows):
+def exchange(block, top_rows, coarse_tops):
     domains, subs = lax.axis_size("dom"), lax.axis_size("sub")
     vmem = pl.BlockSpec(memory_space=pltpu.VMEM)
+    rows, cells = block.shape
     return pl.pallas_call(
         functools.partial(exchange_kernel, domains, subs),
         in_specs=[vmem, vmem],
-        out_specs=[vmem] * 3,
+        out_specs=[vmem] * 2,
         out_shape=[
-            jax.ShapeDtypeStruct(block.shape, jnp.float32),
-            jax.ShapeDtypeStruct(block.shape, jnp.float32),
-            jax.ShapeDtypeStruct((domains,) + top_rows.shape, jnp.float32),
+            jax.ShapeDtypeStruct((rows, 3 * cells), jnp.float32),
+            jax.ShapeDtypeStruct((coarse_tops, top_rows.shape[1]), jnp.float32),
         ],
         scratch_shapes=[
-            pltpu.VMEM(block.shape, jnp.float32),
-            pltpu.VMEM(block.shape, jnp.float32),
+            pltpu.VMEM((3, subs) + block.shape, jnp.float32),
             pltpu.VMEM((domains * subs,) + top_rows.shape, jnp.float32),
-            pltpu.SemaphoreType.DMA((2,)),
-            pltpu.SemaphoreType.DMA((2,)),
+            pltpu.SemaphoreType.DMA((3, subs)),
+            pltpu.SemaphoreType.DMA((3, subs)),
             pltpu.SemaphoreType.DMA,
             pltpu.SemaphoreType.DMA,
             pltpu.SemaphoreType.DMA,
@@ -258,10 +352,34 @@
     )(block, top_rows)
 
 
-def upward(moments, upward_ops):
-    parents = moments.shape[1] // 8
-    grouped = moments.reshape(moments.shape[0], parents, 8)
-    return jnp.einsum("oab,bpo->ap", upward_ops, grouped, precision=precise)
+def prepare(partial, upward_ops, fine_list, mid_list, top_list, upper_list, rows, depth, counts):
+    coeffs, cells = partial.shape
+    top_cells = top_list.shape[1]
+    vmem = pl.BlockSpec(memory_space=pltpu.VMEM)
+
+    return pl.pallas_call(
+        functools.partial(prepare_kernel, counts),
+        in_specs=[vmem] * 6,
+        out_specs=[vmem] * 4,
+        out_shape=[
+            jax.ShapeDtypeStruct((rows, cells), jnp.float32),
+            jax.ShapeDtypeStruct((top_cells, 2 * LANES), jnp.float32),
+            jax.ShapeDtypeStruct((depth, LANES), jnp.int32),
+            jax.ShapeDtypeStruct((depth, LANES), jnp.int32),
+        ],
+        scratch_shapes=[
+            pltpu.VMEM((rows, 8, 2 * LANES), jnp.float32),
+            pltpu.VMEM((LANES, LANES), jnp.float32),
+        ],
+        compiler_params=pltpu.CompilerParams(vmem_limit_bytes=32 * 1024 * 1024),
+    )(
+        partial,
+        jnp.transpose(upward_ops, (1, 0, 2)),
+        fine_list,
+        jnp.transpose(mid_list),
+        jnp.transpose(top_list),
+        jnp.transpose(upper_list),
+    )
 
 
 def downward(expansions, downward_ops):
@@ -299,21 +417,15 @@
     rows = round_up(coeffs, 24)
     depth = round_up(slots, 16)
     upper_span = max(1, top_cells // 8)
-    upper_first = domain * top_cells // 8
-    upper_sources = lax.dynamic_slice_in_dim(upper_list, upper_first, upper_span, 1)
-
-    partial = fine_partial[0]
-    own_top = upward(upward(partial, upward_ops), upward_ops)
-    top_rows = jnp.pad(jnp.transpose(own_top), ((0, 0), (0, 2 * LANES - coeffs)))
-    block = jnp.pad(settle(partial), ((0, rows - coeffs), (0, 0)))
-    low, high, tops = exchange(block, top_rows)
-    wide_fine = jnp.concatenate([low, block, high], axis=1)
-    wide_mid = upward(wide_fine[:coeffs], upward_ops)
-    top_moments = jnp.transpose(tops.reshape(-1, 2 * LANES)[:, :coeffs])
-    upper_moments = upward(top_moments, upward_ops)
-
-    def place(sources, offset):
-        return jnp.where(sources >= 0, sources + offset, -1)
+    spread = 3 * mid_cells
+    tops = top_cells * lax.axis_size("dom")
+    coarse_width = round_up(spread + tops + tops // 8, LANES)
+    counts = (slab_cells, mid_cells, top_cells, spread, tops)
+    block, top_rows, fine_sources, coarse_sources = prepare(
+        fine_partial[0], upward_ops, fine_list, mid_list, top_list, upper_list,
+        rows, depth, counts,
+    )
+    wide_fine, top_moments = exchange(block, top_rows, round_up(tops, LANES))
 
     def padded(array, height, width, fill):
         return jnp.pad(
@@ -322,23 +434,9 @@
             constant_values=fill,
         )
 
-    spread = wide_mid.shape[1]
-    coarse = jnp.concatenate([wide_mid, top_moments, upper_moments], axis=1)
-    coarse_sources = jnp.concatenate(
-        [
-            place(mid_list, mid_cells - domain * mid_cells),
-            place(top_list, spread),
-            place(upper_sources, spread + top_moments.shape[1]),
-        ],
-        axis=1,
-    )
-    fine_sources = place(fine_list, slab_cells - domain * slab_cells)
     terms = interact(
-        wide_fine,
-        padded(coarse, rows, round_up(coarse.shape[1], LANES), 0),
-        padded(fine_sources, depth, LANES, -1),
-        padded(coarse_sources, depth, LANES, -1),
-        jnp.transpose(interaction_ops, (1, 2, 0)),
+        wide_fine, top_moments, upward_ops, fine_sources, coarse_sources,
+        jnp.transpose(interaction_ops, (1, 2, 0)), spread, tops, coarse_width,
     )
     terms = settle(terms)[:coeffs]
     at = LANES

time: 64.5 us -> 67.6 us (1.048)
  Pallas kernels: 34.9 us -> 47.7 us
  matrix products: 10.4 us -> 3.17 us
  local copies, waits for them, and re-layouts: 4.17 us -> 8.67 us
  other arithmetic: 4.3 us -> 0.29 us
  starting transfers between devices: 4.19 us -> 1.12 us
    dot_general x4 -> x0, matrix products: 7.1 us -> none  [upward(): return jnp.einsum('oab,bpo->ap', upward_ops, grouped, precision=precise)]
    pallas_call x1, Pallas kernels: 11 us -> 17.5 us  [exchange(): pl.pallas_call(functools.partial(exchange_kernel, domains, subs), in_spec...]
    pallas_call x1 -> x2, Pallas kernels: 21.4 us -> 27.6 us  [the longest x1 24.3 us: interact(): pl.pallas_call(functools.partial(interact_kernel, coeffs, slots, group, s...]
    unnamed x19 -> x31, local copies, waits for them, and re-layouts: 2.14 us -> 8.2 us
    ppermute x2 -> x1, starting transfers between devices: 4.19 us -> 1.12 us  [settle(): moving = lax.ppermute(moving, 'sub', ring)]
    select_n x4 -> x0, other arithmetic: 2.88 us -> none  [place(): return jnp.where(sources >= 0, sources + offset, -1)]
    pad x2 -> x0, local copies, waits for them, and re-layouts: 1.25 us -> none  [the longest x1 0.64 us: shards(): block = jnp.pad(settle(partial), ((0, rows - coeffs), (0, 0)))]
    concatenate x3 -> x0, other arithmetic: 1.12 us -> none  [the longest x1 0.99 us: shards(): wide_fine = jnp.concatenate([low, block, high], axis=1)]
  transfers between devices with their start and end apart: 2 -> 1, of which waited for: 1 -> 1; matrix products, arithmetic and copies ran while one was open for 14% -> 0% of each run, Pallas kernels for 0% -> 0%
where the time goes in v3:
time: 67.6 us; the launch traced here: 67 us
  Pallas kernels  47.7 us (71%)
  local copies, waits for them, and re-layouts  8.67 us (13%)
  waiting for transfers between devices  5.33 us (8%)
  matrix products  3.17 us (5%)
  starting transfers between devices  1.12 us (2%)
  between operations  0.77 us (1%)
    pallas_call x1, Pallas kernels, interact(): pl.pallas_call(functools.partial(interact_kernel, coeffs, slots, group, s...  24.3 us
    pallas_call x1, Pallas kernels, exchange(): pl.pallas_call(functools.partial(exchange_kernel, domains, subs), in_spec...  17.5 us
    unnamed x31, local copies, waits for them, and re-layouts  8.2 us
    ppermute x1, waiting for transfers between devices, settle(): moving = lax.ppermute(moving, 'sub', ring)  5.33 us
    pallas_call x1, Pallas kernels, prepare(): pl.pallas_call(functools.partial(prepare_kernel, counts), in_specs=[vmem]...  3.36 us
    dot_general x2, matrix products, downward(): jnp.einsum('oab,bp->apo', downward_ops, expansions, precision=precise)  3.17 us
    pallas_call x1, Pallas kernels, evaluate(): pl.pallas_call(potential_kernel, out_shape=jax.ShapeDtypeStruct((1, leave...  2.54 us
  transfers between devices with their start and end apart: 1, of which 1 were waited for; matrix products, arithmetic and copies ran while one was open for 0% of the time, Pallas kernels for 0%

profile of v3, /device:TPU:0, one launch (start us, length us, event | category | flops | bytes accessed | tf_op | source)
XLA Modules:
  0.0 67.0 jit_solution(8759872995031794262)
XLA Ops:
  0.6 0.9 %copy.56 = f32[1,165,128]{2,1,0:T(8,128)S(1)} copy(f32[1,165,128]{2,0,1:T(1,128)} %param.11) | data formatting | bytes 168960
  1.5 1.3 %copy-done = f32[8,165,165]{2,0,1:T(8,128)S(1)} copy-done((f32[8,165,165]{2,0,1:T(8,128)S(1)}, f32[8,165,165]{2,0,1:T(8,128)}, u32[]{:S(2)}) %copy-start) | copy-done | bytes 871224
  2.9 0.8 %copy-done.4 = s32[94,128]{1,0:T(8,128)S(1)} copy-done((s32[94,128]{1,0:T(8,128)S(1)}, s32[94,128]{1,0:T(8,128)}, u32[]{:S(2)}) %copy-start.4) | copy-done | bytes 48152
  3.7 0.7 %copy-done.6 = s32[94,16]{0,1:T(8,128)S(1)} copy-done((s32[94,16]{0,1:T(8,128)S(1)}, s32[94,16]{0,1:T(8,128)}, u32[]{:S(2)}) %copy-start.6) | copy-done | bytes 6040
  4.4 0.7 %copy-done.7 = s32[94,4]{0,1:T(4,128)S(1)} copy-done((s32[94,4]{0,1:T(4,128)S(1)}, s32[94,4]{0,1:T(4,128)}, u32[]{:S(2)}) %copy-start.7) | copy-done | bytes 1528
  5.0 0.7 %copy-done.9 = s32[94,2]{0,1:T(2,128)S(1)} copy-done((s32[94,2]{0,1:T(2,128)S(1)}, s32[94,2]{0,1:T(2,128)}, u32[]{:S(2)}) %copy-start.9) | copy-done | bytes 776
  5.7 3.4 %shard_map.122 = (f32[168,128]{1,0:T(8,128)S(1)}, f32[2,256]{1,0:T(2,128)S(1)}, s32[96,128]{1,0:T(8,128)S(1)}, s32[96,128]{1,0:T(8,128)S(1)}) custom-call(f32[165,128]{1,0:T(8,128)S(1)} %bitcast.39, f32[165,8,165]{2,1,0:T(8,128)S(1)} %bitcast.37, s32[94,128]{1,0:T(8,128)S(1)} %copy-done.4, s32[16,94]{1,0:T(8,128)S(1)} %bitcast.41, s32[2,94]{1,0:T(2,128)S(1)} %bitcast.43, ...), custom_call_target="tpu_custom_call" | custom-call | tf_op jit(solution)/shard_map/pallas_call | solution.py:360
  9.1 0.7 copy-done.3
  9.7 0.6 copy-done.8
  10.3 17.5 %shard_map.123 = (f32[168,384]{1,0:T(8,128)}, f32[128,256]{1,0:T(8,128)}) custom-call(f32[168,128]{1,0:T(8,128)} %copy-done.3, f32[2,256]{1,0:T(2,128)} %copy-done.8), custom_call_target="tpu_custom_call" | custom-call | tf_op jit(solution)/shard_map/pallas_call | solution.py:334
  27.9 0.0 copy-done.1
  27.9 0.0 copy-start.10
  27.9 0.9 %copy-done.10 = f32[168,384]{1,0:T(8,128)S(1)} copy-done((f32[168,384]{1,0:T(8,128)S(1)}, f32[168,384]{1,0:T(8,128)}, u32[]{:S(2)}) %copy-start.10) | copy-done | bytes 258072
  28.8 0.9 %copy-done.11 = f32[128,256]{1,0:T(8,128)S(1)} copy-done((f32[128,256]{1,0:T(8,128)S(1)}, f32[128,256]{1,0:T(8,128)}, u32[]{:S(2)}) %copy-start.11) | copy-done | bytes 131096
  29.7 24.3 %shard_map.124 = f32[168,256]{1,0:T(8,128)S(1)} custom-call(f32[168,384]{1,0:T(8,128)S(1)} %copy-done.10, f32[128,256]{1,0:T(8,128)S(1)} %copy-done.11, f32[165,8,165]{2,1,0:T(8,128)S(1)} %bitcast.38, s32[96,128]{1,0:T(8,128)S(1)} %get-tuple-element.12.fine_list, s32[96,128]{1,0:T(8,128)S(1)} %get-tuple-element.13.coarse_list, f32[165,165,94]{2,1,0:T(8,128)} %bitcast.47), custom_call_target="tpu_custom_call" | custom-call | flops 5549064192 | bytes 14450688 | tf_op jit(solution)/shard_map/pallas_call | solution.py:123
  54.0 1.1 %collective-permute-start = (f32[168,256]{1,0:T(8,128)S(1)}, f32[168,256]{1,0:T(8,128)S(1)}, u32[]{:S(2)}, u32[]{:S(2)}) collective-permute-start(f32[168,256]{1,0:T(8,128)S(1)} %shard_map.124), channel_id=1, source_target_pairs={{0,1},{1,0},{2,3},{3,2},{4,5},{5,4},{6,7},{7,6},{8,9},{9,8},{10,11... | collective-permute-start | bytes 516104 | tf_op jit(solution)/shard_map/ppermute | solution.py:395
  55.1 0.0 copy-done.14
  55.1 5.3 %collective-permute-done = f32[168,256]{1,0:T(8,128)S(1)} collective-permute-done((f32[168,256]{1,0:T(8,128)S(1)}, f32[168,256]{1,0:T(8,128)S(1)}, u32[]{:S(2)}, u32[]{:S(2)}) %collective-permute-start) | collective-permute-done | bytes 172064 | tf_op jit(solution)/shard_map/ppermute | solution.py:395
  60.5 0.2 slice_reduce_fusion
  60.7 0.0 copy-done.12
  60.7 0.3 multiply_reduce_fusion
  60.9 1.6 %fusion.7 = f32[165,2,8]{0,1,2:T(2,128)S(1)} fusion(f32[8,165,165]{2,0,1:T(8,128)S(1)} %copy-done.12, f32[168,256]{1,0:T(8,128)S(1)} %add.23, f32[8,165]{0,1:T(8,128)S(1)} %multiply_reduce_fusion, s32[]{:T(128)S(6)} %select_n.11), kind=kOutput, calls=%fused_computation.6 | convolution fusion | flops 5227530 | bytes 1534276 | tf_op jit(solution)/shard_map/oab,bp->apo/dot_general | solution.py:386
  62.6 0.0 copy-start.2
  62.6 0.0 copy-start.5
  62.6 0.1 copy.30
  62.7 1.6 %fusion.4 = f32[165,16,8]{0,1,2:T(8,128)S(1)} fusion(f32[8,165,165]{2,0,1:T(8,128)S(1)} %copy-done.12, f32[165,16]{1,0:T(8,128)S(1)} %copy.30, f32[168,256]{1,0:T(8,128)S(1)} %add.23), kind=kOutput, calls=%fused_computation.5 | convolution fusion | flops 41820240 | bytes 1608192 | tf_op jit(solution)/shard_map/oab,bp->apo/dot_general | solution.py:386
  64.2 0.1 copy.55
  64.3 0.1 copy.34
  64.5 0.0 copy-start.13
  64.5 0.0 copy-done.2
  64.5 2.5 %shard_map.125 = f32[1,2048]{1,0:T(1,128)} custom-call(f32[168,128]{1,0:T(8,128)S(1)} %pad.8.local_ref, s32[1,2048]{1,0:T(1,128)S(1)} %bitcast.40, f32[3,2048]{1,0:T(4,128)S(1)} %copy-done.5, s32[168,128]{1,0:T(8,128)S(1)} %copy-done.2), custom_call_target="tpu_custom_call" | custom-call | tf_op jit(solution)/shard_map/pallas_call | solution.py:178
  67.0 0.0 copy-done.13
  (17 shorter events, 0.1 us)
Async XLA Ops:
  1.5 1.3 %copy-start = (f32[8,165,165]{2,0,1:T(8,128)S(1)}, f32[8,165,165]{2,0,1:T(8,128)}, u32[]{:S(2)}) copy-start(f32[8,165,165]{2,0,1:T(8,128)} %param.12) | copy-start | bytes 2613604
  2.9 0.8 %copy-start.4 = (s32[94,128]{1,0:T(8,128)S(1)}, s32[94,128]{1,0:T(8,128)}, u32[]{:S(2)}) copy-start(s32[94,128]{1,0:T(8,128)} %fine_ref.1) | copy-start | bytes 144388
  3.7 0.7 %copy-start.6 = (s32[94,16]{0,1:T(8,128)S(1)}, s32[94,16]{0,1:T(8,128)}, u32[]{:S(2)}) copy-start(s32[94,16]{0,1:T(8,128)} %param.16) | copy-start | bytes 18052
  4.4 0.7 %copy-start.7 = (s32[94,4]{0,1:T(4,128)S(1)}, s32[94,4]{0,1:T(4,128)}, u32[]{:S(2)}) copy-start(s32[94,4]{0,1:T(4,128)} %param.18) | copy-start | bytes 4516
  5.0 0.7 %copy-start.9 = (s32[94,2]{0,1:T(2,128)S(1)}, s32[94,2]{0,1:T(2,128)}, u32[]{:S(2)}) copy-start(s32[94,2]{0,1:T(2,128)} %param.17) | copy-start | bytes 2260
  5.7 22.1 %copy-start.1 = (f32[8,165,165]{2,0,1:T(8,128)S(1)}, f32[8,165,165]{2,0,1:T(8,128)}, u32[]{:S(2)}) copy-start(f32[8,165,165]{2,0,1:T(8,128)} %param.12) | copy-start | bytes 2613604
  9.1 0.7 copy-start.3
  9.7 0.6 copy-start.8
  27.9 0.9 %copy-start.10 = (f32[168,384]{1,0:T(8,128)S(1)}, f32[168,384]{1,0:T(8,128)}, u32[]{:S(2)}) copy-start(f32[168,384]{1,0:T(8,128)} %get-tuple-element.10.fine_ref) | copy-start | bytes 774148
  28.8 0.9 %copy-start.11 = (f32[128,256]{1,0:T(8,128)S(1)}, f32[128,256]{1,0:T(8,128)}, u32[]{:S(2)}) copy-start(f32[128,256]{1,0:T(8,128)} %get-tuple-element.11.tops_ref) | copy-start | bytes 393220
  29.7 25.4 %copy-start.14 = (s32[2048]{0:T(1024)S(1)}, s32[2048]{0:T(1024)}, u32[]{:S(2)}) copy-start(s32[2048]{0:T(1024)} %param.20) | copy-start | bytes 24580
  29.7 31.0 %copy-start.12 = (f32[8,165,165]{2,0,1:T(8,128)S(1)}, f32[8,165,165]{2,0,1:T(8,128)}, u32[]{:S(2)}) copy-start(f32[8,165,165]{2,0,1:T(8,128)} %param.14) | copy-start | bytes 2613604
  54.0 6.5 %collective-permute-start = (f32[168,256]{1,0:T(8,128)S(1)}, f32[168,256]{1,0:T(8,128)S(1)}, u32[]{:S(2)}, u32[]{:S(2)}) collective-permute-start(f32[168,256]{1,0:T(8,128)S(1)} %shard_map.124), channel_id=1, source_target_pairs={{0,1},{1,0},{2,3},{3,2},{4,5},{5,4},{6,7},{7,6},{8,9},{9,8},{10,11... | collective-permute-start | bytes 516104 | tf_op jit(solution)/shard_map/ppermute | solution.py:395
  62.6 1.9 %copy-start.2 = (s32[168,128]{1,0:T(8,128)S(1)}, s32[168,128]{1,0:T(8,128)}, u32[]{:S(2)}) copy-start(s32[168,128]{1,0:T(8,128)} %constant.36.exponent_ref) | copy-start | bytes 258052
  62.6 1.9 %copy-start.5 = (f32[3,2048]{1,0:T(4,128)S(1)}, f32[3,2048]{1,0:T(4,128)}, u32[]{:S(2)}) copy-start(f32[3,2048]{1,0:T(4,128)} %position_ref.1) | copy-start | bytes 73732
  64.5 2.6 %copy-start.13 = (f32[165,128]{1,0:T(8,128)}, f32[165,128]{1,0:T(8,128)S(1)}, u32[]{:S(2)}) copy-start(f32[165,128]{1,0:T(8,128)S(1)} %slice_add_fusion.2) | copy-start | bytes 253444

commit v4 on v3

--- a/solution.py
+++ b/solution.py
@@ -212,19 +212,19 @@
     return halves(jnp.concatenate([ops[o] for o in range(8)], axis=1))
 
 
-def prepare_kernel(
+def prepare(
     counts, partial_ref, upward_ref, fine_ref, mid_ref, top_ref, upper_ref,
-    block_out, rows_out, fine_out, coarse_out, held, lists,
+    rows_out, fine_out, coarse_out, held, lists,
 ):
-    rows = block_out.shape[0]
+    rows = held.shape[0]
     coeffs = partial_ref.shape[0]
     slots = fine_ref.shape[0]
     slab, mid, top, spread, tops = counts
     domain = lax.axis_index("dom")
-    block_out[...] = jnp.zeros_like(block_out)
-    block_out[:coeffs, :] = partial_ref[...]
+    filler = jnp.zeros((rows - coeffs, partial_ref.shape[1]), jnp.float32)
+    block = jnp.concatenate([partial_ref[...], filler], axis=0)
     high, low = split_upward(upward_ref, held)
-    top_moments = raise_level(raise_level(block_out[...], high, low), high, low)
+    top_moments = raise_level(raise_level(block, high, low), high, low)
     filler = jnp.zeros((2 * LANES - rows, LANES), jnp.float32)
     turned = jnp.transpose(jnp.concatenate([top_moments, filler], axis=0))
     rows_out[...] = turned[: rows_out.shape[0]]
@@ -248,14 +248,15 @@
 
 
 def exchange_kernel(
-    domains, subs, block_ref, top_ref, wide_out, tops_out,
-    sides, tops, side_send, side_recv, top_send, top_recv, own_sem,
+    domains, subs, counts, block_ref, partial_ref, upward_ref, fine_ref, mid_ref, top_list_ref,
+    upper_ref, wide_out, tops_out, fine_out, coarse_out,
+    low, high, tops, top_ref, held, lists, side_send, side_recv, top_send, top_recv,
 ):
     domain, sub = lax.axis_index("dom"), lax.axis_index("sub")
     count = domains * subs
     flat = domain * subs + sub
     mesh = pl.DeviceIdType.MESH
-    cells = block_ref.shape[1]
+    coeffs, cells = block_ref.shape
     top_cells = top_ref.shape[0]
 
     def peer(offset):
@@ -269,27 +270,15 @@
         return carry
 
     lax.fori_loop(1, count, greet, 0)
-    own = pltpu.make_async_copy(top_ref, tops.at[count - 1], own_sem)
-    own.start()
+    prepare(
+        counts, partial_ref, upward_ref, fine_ref, mid_ref, top_list_ref, upper_ref,
+        top_ref, fine_out, coarse_out, held, lists,
+    )
+    tops[count - 1] = top_ref[...]
+    tops_out[...] = jnp.zeros_like(tops_out)
+    wide_out[...] = jnp.zeros_like(wide_out)
+    wide_out[:coeffs, cells : 2 * cells] = block_ref[...]
     pl.semaphore_wait(barrier, count - 1)
-    copies = []
-    for turn in range(subs):
-        for index, move in enumerate((1, domains - 1, 0)):
-            if turn == 0 and move == 0:
-                continue
-            side = pltpu.make_async_remote_copy(
-                src_ref=block_ref,
-                dst_ref=sides.at[index, turn],
-                send_sem=side_send.at[index, turn],
-                recv_sem=side_recv.at[index, turn],
-                device_id={
-                    "dom": lax.rem(domain + move, domains),
-                    "sub": lax.rem(sub + turn, subs),
-                },
-                device_id_type=mesh,
-            )
-            side.start()
-            copies.append(side)
 
     def send(offset, carry):
         pltpu.make_async_remote_copy(
@@ -303,10 +292,20 @@
         return carry
 
     lax.fori_loop(1, count, send, 0)
-    own.wait()
+    copies = []
+    for index, (target, move) in enumerate(((low, 1), (high, domains - 1))):
+        side = pltpu.make_async_remote_copy(
+            src_ref=block_ref,
+            dst_ref=target,
+            send_sem=side_send.at[index],
+            recv_sem=side_recv.at[index],
+            device_id={"dom": lax.rem(domain + move, domains), "sub": sub},
+            device_id_type=mesh,
+        )
+        side.start()
+        copies.append(side)
     arrived = tops.at[pl.ds(0, count - 1)]
     pltpu.make_async_copy(arrived, arrived, top_recv).wait()
-    tops_out[...] = jnp.zeros_like(tops_out)
 
     def gather(offset, carry):
         source = lax.rem(flat + count - offset, count) // subs
@@ -319,60 +318,43 @@
     lax.fori_loop(0, count, gather, 0)
     for side in copies:
         side.wait()
-    for index, start in ((0, 0), (2, cells), (1, 2 * cells)):
-        held = [block_ref[...]] if index == 2 else [sides[index, 0]]
-        for turn in range(1, subs):
-            held.append(sides[index, turn])
-        wide_out[:, start : start + cells] = sum(held[1:], held[0])
+    wide_out[:coeffs, :cells] = low[...]
+    wide_out[:coeffs, 2 * cells :] = high[...]
     pltpu.make_async_copy(arrived, arrived, top_send).wait()
 
 
-def exchange(block, top_rows, coarse_tops):
+def exchange(block, partial, upward_ops, fine_list, mid_list, top_list, upper_list, rows, depth, counts):
     domains, subs = lax.axis_size("dom"), lax.axis_size("sub")
+    coeffs, cells = block.shape
+    top_cells = top_list.shape[1]
     vmem = pl.BlockSpec(memory_space=pltpu.VMEM)
-    rows, cells = block.shape
     return pl.pallas_call(
-        functools.partial(exchange_kernel, domains, subs),
-        in_specs=[vmem, vmem],
-        out_specs=[vmem] * 2,
+        functools.partial(exchange_kernel, domains, subs, counts),
+        in_specs=[vmem] * 7,
+        out_specs=[vmem] * 4,
         out_shape=[
             jax.ShapeDtypeStruct((rows, 3 * cells), jnp.float32),
-            jax.ShapeDtypeStruct((coarse_tops, top_rows.shape[1]), jnp.float32),
-        ],
-        scratch_shapes=[
-            pltpu.VMEM((3, subs) + block.shape, jnp.float32),
-            pltpu.VMEM((domains * subs,) + top_rows.shape, jnp.float32),
-            pltpu.SemaphoreType.DMA((3, subs)),
-            pltpu.SemaphoreType.DMA((3, subs)),
-            pltpu.SemaphoreType.DMA,
-            pltpu.SemaphoreType.DMA,
-            pltpu.SemaphoreType.DMA,
-        ],
-        compiler_params=pltpu.CompilerParams(collective_id=0, has_side_effects=True),
-    )(block, top_rows)
-
-
-def prepare(partial, upward_ops, fine_list, mid_list, top_list, upper_list, rows, depth, counts):
-    coeffs, cells = partial.shape
-    top_cells = top_list.shape[1]
-    vmem = pl.BlockSpec(memory_space=pltpu.VMEM)
-
-    return pl.pallas_call(
-        functools.partial(prepare_kernel, counts),
-        in_specs=[vmem] * 6,
-        out_specs=[vmem] * 4,
-        out_shape=[
-            jax.ShapeDtypeStruct((rows, cells), jnp.float32),
-            jax.ShapeDtypeStruct((top_cells, 2 * LANES), jnp.float32),
+            jax.ShapeDtypeStruct((round_up(counts[4], LANES), 2 * LANES), jnp.float32),
             jax.ShapeDtypeStruct((depth, LANES), jnp.int32),
             jax.ShapeDtypeStruct((depth, LANES), jnp.int32),
         ],
         scratch_shapes=[
+            pltpu.VMEM(block.shape, jnp.float32),
+            pltpu.VMEM(block.shape, jnp.float32),
+            pltpu.VMEM((domains * subs, top_cells, 2 * LANES), jnp.float32),
+            pltpu.VMEM((top_cells, 2 * LANES), jnp.float32),
             pltpu.VMEM((rows, 8, 2 * LANES), jnp.float32),
             pltpu.VMEM((LANES, LANES), jnp.float32),
+            pltpu.SemaphoreType.DMA((2,)),
+            pltpu.SemaphoreType.DMA((2,)),
+            pltpu.SemaphoreType.DMA,
+            pltpu.SemaphoreType.DMA,
         ],
-        compiler_params=pltpu.CompilerParams(vmem_limit_bytes=32 * 1024 * 1024),
+        compiler_params=pltpu.CompilerParams(
+            collective_id=0, has_side_effects=True, vmem_limit_bytes=32 * 1024 * 1024
+        ),
     )(
+        block,
         partial,
         jnp.transpose(upward_ops, (1, 0, 2)),
         fine_list,
@@ -421,11 +403,11 @@
     tops = top_cells * lax.axis_size("dom")
     coarse_width = round_up(spread + tops + tops // 8, LANES)
     counts = (slab_cells, mid_cells, top_cells, spread, tops)
-    block, top_rows, fine_sources, coarse_sources = prepare(
-        fine_partial[0], upward_ops, fine_list, mid_list, top_list, upper_list,
+    partial = fine_partial[0]
+    wide_fine, top_moments, fine_sources, coarse_sources = exchange(
+        settle(partial), partial, upward_ops, fine_list, mid_list, top_list, upper_list,
         rows, depth, counts,
     )
-    wide_fine, top_moments = exchange(block, top_rows, round_up(tops, LANES))
 
     def padded(array, height, width, fill):
         return jnp.pad(

time: 67.6 us -> 62.2 us (0.920)
  Pallas kernels: 47.7 us -> 38.9 us
  local copies, waits for them, and re-layouts: 8.67 us -> 5.58 us
  waiting for transfers between devices: 5.33 us -> 8.31 us
  starting transfers between devices: 1.12 us -> 3.64 us
  other arithmetic: 0.29 us -> 1.19 us
    pallas_call x2 -> x1, Pallas kernels: 20.9 us -> 12.1 us  [exchange(): pl.pallas_call(functools.partial(exchange_kernel, domains, subs, counts),...]
    unnamed x31 -> x23, local copies, waits for them, and re-layouts: 8.2 us -> 5.11 us
    ppermute x1 -> x2, waiting for transfers between devices: 5.33 us -> 8.31 us  [settle(): moving = lax.ppermute(moving, 'sub', ring)]
    ppermute x1 -> x2, starting transfers between devices: 1.12 us -> 3.64 us  [settle(): moving = lax.ppermute(moving, 'sub', ring)]
    add x1 -> x2, other arithmetic: 0.03 us -> 0.92 us  [settle(): total = total + moving]
  transfers between devices with their start and end apart: 1 -> 2, of which waited for: 1 -> 2; matrix products, arithmetic and copies ran while one was open for 0% -> 0% of each run, Pallas kernels for 0% -> 0%
where the time goes in v4:
time: 62.2 us; the launch traced here: 61.7 us
  Pallas kernels  38.9 us (63%)
  waiting for transfers between devices  8.31 us (13%)
  local copies, waits for them, and re-layouts  5.58 us (9%)
  starting transfers between devices  3.64 us (6%)
  matrix products  3.26 us (5%)
  other arithmetic  1.19 us (2%)
  between operations  0.78 us (1%)
    pallas_call x1, Pallas kernels, interact(): pl.pallas_call(functools.partial(interact_kernel, coeffs, slots, group, s...  24.3 us
    pallas_call x1, Pallas kernels, exchange(): pl.pallas_call(functools.partial(exchange_kernel, domains, subs, counts),...  12.1 us
    ppermute x2, waiting for transfers between devices, settle(): moving = lax.ppermute(moving, 'sub', ring)  8.31 us
    unnamed x23, local copies, waits for them, and re-layouts  5.11 us
    ppermute x2, starting transfers between devices, settle(): moving = lax.ppermute(moving, 'sub', ring)  3.64 us
    dot_general x2, matrix products, downward(): jnp.einsum('oab,bp->apo', downward_ops, expansions, precision=precise)  3.26 us
    pallas_call x1, Pallas kernels, evaluate(): pl.pallas_call(potential_kernel, out_shape=jax.ShapeDtypeStruct((1, leave...  2.54 us
  transfers between devices with their start and end apart: 2, of which 2 were waited for; matrix products, arithmetic and copies ran while one was open for 0% of the time, Pallas kernels for 0%

profile of v4, /device:TPU:0, one launch (start us, length us, event | category | flops | bytes accessed | tf_op | source)
XLA Modules:
  0.0 61.7 jit_solution(17702831554189748802)
XLA Ops:
  0.6 0.9 %copy.58 = f32[1,165,128]{2,1,0:T(8,128)S(1)} copy(f32[1,165,128]{2,0,1:T(1,128)} %param.11) | data formatting | bytes 168960
  1.5 3.0 %collective-permute-start = (f32[165,128]{1,0:T(8,128)S(1)}, f32[165,128]{1,0:T(8,128)S(1)}, u32[]{:S(2)}, u32[]{:S(2)}) collective-permute-start(f32[165,128]{1,0:T(8,128)S(1)} %bitcast.41), channel_id=1, source_target_pairs={{0,1},{1,0},{2,3},{3,2},{4,5},{5,4},{6,7},{7,6},{8,9},{9,8},{10,11... | collective-permute-start | bytes 253448 | tf_op jit(solution)/shard_map/ppermute | solution.py:377
  4.5 2.5 %collective-permute-done = f32[165,128]{1,0:T(8,128)S(1)} collective-permute-done((f32[165,128]{1,0:T(8,128)S(1)}, f32[165,128]{1,0:T(8,128)S(1)}, u32[]{:S(2)}, u32[]{:S(2)}) %collective-permute-start) | collective-permute-done | bytes 84512 | tf_op jit(solution)/shard_map/ppermute | solution.py:377
  7.0 0.9 %fusion.17.block_ref = f32[165,128]{1,0:T(8,128)S(1)} fusion(f32[165,128]{1,0:T(8,128)S(1)} %collective-permute-done, f32[1,165,128]{2,0,1:T(1,128)} %param.11), kind=kLoop, calls=%fused_computation.20 | loop fusion | flops 21120 | bytes 253440 | tf_op jit(solution)/shard_map/add | solution.py:378
  7.9 0.0 copy-start
  7.9 1.3 %copy-done = f32[8,165,165]{2,0,1:T(8,128)S(1)} copy-done((f32[8,165,165]{2,0,1:T(8,128)S(1)}, f32[8,165,165]{2,0,1:T(8,128)}, u32[]{:S(2)}) %copy-start) | copy-done | bytes 871224
  9.3 0.8 %copy-done.3 = s32[94,128]{1,0:T(8,128)S(1)} copy-done((s32[94,128]{1,0:T(8,128)S(1)}, s32[94,128]{1,0:T(8,128)}, u32[]{:S(2)}) %copy-start.3) | copy-done | bytes 48152
  10.1 0.7 %copy-done.5 = s32[94,16]{0,1:T(8,128)S(1)} copy-done((s32[94,16]{0,1:T(8,128)S(1)}, s32[94,16]{0,1:T(8,128)}, u32[]{:S(2)}) %copy-start.5) | copy-done | bytes 6040
  10.8 0.7 %copy-done.6 = s32[94,4]{0,1:T(4,128)S(1)} copy-done((s32[94,4]{0,1:T(4,128)S(1)}, s32[94,4]{0,1:T(4,128)}, u32[]{:S(2)}) %copy-start.6) | copy-done | bytes 1528
  11.4 0.7 %copy-done.7 = s32[94,2]{0,1:T(2,128)S(1)} copy-done((s32[94,2]{0,1:T(2,128)S(1)}, s32[94,2]{0,1:T(2,128)}, u32[]{:S(2)}) %copy-start.7) | copy-done | bytes 776
  12.1 12.1 %shard_map.122 = (f32[168,384]{1,0:T(8,128)S(1)}, f32[128,256]{1,0:T(8,128)S(1)}, s32[96,128]{1,0:T(8,128)S(1)}, s32[96,128]{1,0:T(8,128)S(1)}) custom-call(f32[165,128]{1,0:T(8,128)S(1)} %fusion.17.block_ref, f32[165,128]{1,0:T(8,128)S(1)} %bitcast.42, f32[165,8,165]{2,1,0:T(8,128)S(1)} %bitcast.39, s32[94,128]{1,0:T(8,128)S(1)} %copy-done.3, ...), custom_call_target="tpu_custom_call" | custom-call | tf_op jit(solution)/shard_map/pallas_call | solution.py:331
  24.2 0.0 copy-done.1
  24.2 0.0 copy-start.10
  24.2 0.0 copy-start.8
  24.3 24.3 %shard_map.123 = f32[168,256]{1,0:T(8,128)S(1)} custom-call(f32[168,384]{1,0:T(8,128)S(1)} %get-tuple-element.6.fine_ref, f32[128,256]{1,0:T(8,128)S(1)} %get-tuple-element.7.tops_ref, f32[165,8,165]{2,1,0:T(8,128)S(1)} %bitcast.40, s32[96,128]{1,0:T(8,128)S(1)} %get-tuple-element.8.fine_list, s32[96,128]{1,0:T(8,128)S(1)} %get-tuple-element.9.coarse_list, ...), custom_call_target="tpu_custom_call" | custom-call | flops 5549064192 | bytes 14450688 | tf_op jit(solution)/shard_map/pallas_call | solution.py:123
  48.5 0.7 %collective-permute-start.1 = (f32[168,256]{1,0:T(8,128)S(1)}, f32[168,256]{1,0:T(8,128)S(1)}, u32[]{:S(2)}, u32[]{:S(2)}) collective-permute-start(f32[168,256]{1,0:T(8,128)S(1)} %shard_map.123), channel_id=1, source_target_pairs={{0,1},{1,0},{2,3},{3,2},{4,5},{5,4},{6,7},{7,6},{8,9},{9,8},{10,11... | collective-permute-start | bytes 516104 | tf_op jit(solution)/shard_map/ppermute | solution.py:377
  49.2 0.0 copy-done.10
  49.2 5.8 %collective-permute-done.1 = f32[168,256]{1,0:T(8,128)S(1)} collective-permute-done((f32[168,256]{1,0:T(8,128)S(1)}, f32[168,256]{1,0:T(8,128)S(1)}, u32[]{:S(2)}, u32[]{:S(2)}) %collective-permute-start.1) | collective-permute-done | bytes 172064 | tf_op jit(solution)/shard_map/ppermute | solution.py:377
  55.0 0.2 slice_reduce_fusion
  55.2 0.0 copy-done.8
  55.2 0.3 multiply_reduce_fusion
  55.5 1.7 %fusion.7 = f32[165,2,8]{0,1,2:T(2,128)S(1)} fusion(f32[8,165,165]{2,0,1:T(8,128)S(1)} %copy-done.8, f32[168,256]{1,0:T(8,128)S(1)} %add.27, f32[8,165]{0,1:T(8,128)S(1)} %multiply_reduce_fusion, s32[]{:T(128)S(6)} %select_n.11), kind=kOutput, calls=%fused_computation.6 | convolution fusion | flops 5227530 | bytes 1534276 | tf_op jit(solution)/shard_map/oab,bp->apo/dot_general | solution.py:368
  57.1 0.0 copy-start.2
  57.2 0.0 copy-start.4
  57.2 0.1 copy.30
  57.3 1.6 %fusion.4 = f32[165,16,8]{0,1,2:T(8,128)S(1)} fusion(f32[8,165,165]{2,0,1:T(8,128)S(1)} %copy-done.8, f32[165,16]{1,0:T(8,128)S(1)} %copy.30, f32[168,256]{1,0:T(8,128)S(1)} %add.27), kind=kOutput, calls=%fused_computation.5 | convolution fusion | flops 41820240 | bytes 1608192 | tf_op jit(solution)/shard_map/oab,bp->apo/dot_general | solution.py:368
  58.9 0.1 copy.57
  59.0 0.1 copy.34
  59.1 0.0 copy-start.9
  59.1 0.0 copy-done.2
  59.1 0.0 copy-done.4
  59.1 2.5 %shard_map.124 = f32[1,2048]{1,0:T(1,128)} custom-call(f32[168,128]{1,0:T(8,128)S(1)} %pad.8.local_ref, s32[1,2048]{1,0:T(1,128)S(1)} %bitcast.43, f32[3,2048]{1,0:T(4,128)S(1)} %copy-done.4, s32[168,128]{1,0:T(8,128)S(1)} %copy-done.2), custom_call_target="tpu_custom_call" | custom-call | tf_op jit(solution)/shard_map/pallas_call | solution.py:178
  (11 shorter events, 0.1 us)
Async XLA Ops:
  1.5 5.5 %collective-permute-start = (f32[165,128]{1,0:T(8,128)S(1)}, f32[165,128]{1,0:T(8,128)S(1)}, u32[]{:S(2)}, u32[]{:S(2)}) collective-permute-start(f32[165,128]{1,0:T(8,128)S(1)} %bitcast.41), channel_id=1, source_target_pairs={{0,1},{1,0},{2,3},{3,2},{4,5},{5,4},{6,7},{7,6},{8,9},{9,8},{10,11... | collective-permute-start | bytes 253448 | tf_op jit(solution)/shard_map/ppermute | solution.py:377
  7.9 1.3 %copy-start = (f32[8,165,165]{2,0,1:T(8,128)S(1)}, f32[8,165,165]{2,0,1:T(8,128)}, u32[]{:S(2)}) copy-start(f32[8,165,165]{2,0,1:T(8,128)} %param.12) | copy-start | bytes 2613604
  9.3 0.8 %copy-start.3 = (s32[94,128]{1,0:T(8,128)S(1)}, s32[94,128]{1,0:T(8,128)}, u32[]{:S(2)}) copy-start(s32[94,128]{1,0:T(8,128)} %fine_ref.1) | copy-start | bytes 144388
  10.1 0.7 %copy-start.5 = (s32[94,16]{0,1:T(8,128)S(1)}, s32[94,16]{0,1:T(8,128)}, u32[]{:S(2)}) copy-start(s32[94,16]{0,1:T(8,128)} %param.16) | copy-start | bytes 18052
  10.8 0.7 %copy-start.6 = (s32[94,4]{0,1:T(4,128)S(1)}, s32[94,4]{0,1:T(4,128)}, u32[]{:S(2)}) copy-start(s32[94,4]{0,1:T(4,128)} %param.18) | copy-start | bytes 4516
  11.4 0.7 %copy-start.7 = (s32[94,2]{0,1:T(2,128)S(1)}, s32[94,2]{0,1:T(2,128)}, u32[]{:S(2)}) copy-start(s32[94,2]{0,1:T(2,128)} %param.17) | copy-start | bytes 2260
  12.1 12.1 %copy-start.1 = (f32[8,165,165]{2,0,1:T(8,128)S(1)}, f32[8,165,165]{2,0,1:T(8,128)}, u32[]{:S(2)}) copy-start(f32[8,165,165]{2,0,1:T(8,128)} %param.12) | copy-start | bytes 2613604
  24.2 25.0 %copy-start.10 = (s32[2048]{0:T(1024)S(1)}, s32[2048]{0:T(1024)}, u32[]{:S(2)}) copy-start(s32[2048]{0:T(1024)} %param.20) | copy-start | bytes 24580
  24.2 31.0 %copy-start.8 = (f32[8,165,165]{2,0,1:T(8,128)S(1)}, f32[8,165,165]{2,0,1:T(8,128)}, u32[]{:S(2)}) copy-start(f32[8,165,165]{2,0,1:T(8,128)} %param.14) | copy-start | bytes 2613604
  48.5 6.5 %collective-permute-start.1 = (f32[168,256]{1,0:T(8,128)S(1)}, f32[168,256]{1,0:T(8,128)S(1)}, u32[]{:S(2)}, u32[]{:S(2)}) collective-permute-start(f32[168,256]{1,0:T(8,128)S(1)} %shard_map.123), channel_id=1, source_target_pairs={{0,1},{1,0},{2,3},{3,2},{4,5},{5,4},{6,7},{7,6},{8,9},{9,8},{10,11... | collective-permute-start | bytes 516104 | tf_op jit(solution)/shard_map/ppermute | solution.py:377
  57.1 2.0 %copy-start.2 = (s32[168,128]{1,0:T(8,128)S(1)}, s32[168,128]{1,0:T(8,128)}, u32[]{:S(2)}) copy-start(s32[168,128]{1,0:T(8,128)} %constant.36.exponent_ref) | copy-start | bytes 258052
  57.2 2.0 %copy-start.4 = (f32[3,2048]{1,0:T(4,128)S(1)}, f32[3,2048]{1,0:T(4,128)}, u32[]{:S(2)}) copy-start(f32[3,2048]{1,0:T(4,128)} %position_ref.1) | copy-start | bytes 73732
  59.1 2.6 %copy-start.9 = (f32[165,128]{1,0:T(8,128)}, f32[165,128]{1,0:T(8,128)S(1)}, u32[]{:S(2)}) copy-start(f32[165,128]{1,0:T(8,128)S(1)} %slice_add_fusion.2) | copy-start | bytes 253444
